TPU v7x, 32 devices: a whole 2x2x4 slice. The times are simulated.
32 devices in a mesh: gx: 4 (over x, core), gy: 4 (over z), gz: 2 (over y).
Axes of the slice: x: 2, y: 2, z: 4, core: 2. Of those that a mesh axis runs over, the one named last changes fastest.
Arguments:
- columns: int32 [1024, 2048], P(('gx', 'gy', 'gz')), may hold values from 0 to 32767, as said below
- counts: int32 [1024, 2048], P(('gx', 'gy', 'gz')), may hold values from 1 to 63
- nnz_count: int32 [1024], P(('gx', 'gy', 'gz')), may hold values from 1 to 2048, as said below
- selected: int32 [2048], replicated, may hold values from 0 to 32767, as said below
Outputs:
- gene_stats: float32 [2, 32768], P(None, 'gz')
- pca_input: bfloat16 [1024, 2048], P(('gx', 'gy'), 'gz')
Inputs may be any that keep to these rules, and one draw needn't show every extreme that they name: `columns`: in each row no two slots fall in the same block of 16 consecutive genes (so the first nnz_count slots hold distinct genes); slots beyond nnz_count are not part of the matrix. For every k, the live slots of one cell fall on at most 128 of the genes selected[k * 2048 / 2] to selected[(k + 1) * 2048 / 2 - 1]; some cell reaches 128 for every k in every draw. `nnz_count`: some cell has all 2048 slots live in every draw. `selected`: distinct genes.
All inputs are finite; a program needn't handle non-finite values.
Results may differ from a plain program's by a relative error of at most 0.0085.
Values may be sent and summed in bfloat16 or wider, within the bound.
No kernel may reach another device: no remote copies, remote signals or barrier semaphores. Data moves between devices by JAX's collectives and lax.ppermute only.
A program may use at most 128 MiB of HBM per device.

v0:
```python
import jax
import jax.numpy as jnp
from jax import lax
from jax.sharding import PartitionSpec as P

GENES = 32768
SEL = 2048


target_sum = 10000.0
var_floor = 0.01
clip_value = 10.0
lane_count = 256


def standardize(dense, mean_sel, variance_sel):
    scale_sel = jnp.sqrt(jnp.maximum(variance_sel, var_floor))
    return jnp.clip((dense - mean_sel[None, :]) / scale_sel[None, :], -clip_value, clip_value)


def cell_block(pair):
    block_genes, block_values = pair
    high_count = GENES // lane_count
    high_ids = lax.broadcasted_iota(jnp.int32, (1, 1, high_count), 2)
    low_ids = lax.broadcasted_iota(jnp.int32, (1, 1, lane_count), 2)
    high_table = ((block_genes // lane_count)[:, :, None] == high_ids).astype(jnp.bfloat16)
    low_hit = (block_genes % lane_count)[:, :, None] == low_ids
    upper = lax.optimization_barrier(block_values.astype(jnp.bfloat16))
    lower = (block_values - upper.astype(jnp.float32)).astype(jnp.bfloat16)
    upper_table = jnp.where(low_hit, upper[:, :, None], jnp.bfloat16(0.0))
    lower_table = jnp.where(low_hit, lower[:, :, None], jnp.bfloat16(0.0))
    upper_part = jnp.einsum(
        "csh,csl->chl", high_table, upper_table, preferred_element_type=jnp.float32
    )
    lower_part = jnp.einsum(
        "csh,csl->chl", high_table, lower_table, preferred_element_type=jnp.float32
    )
    return upper_part + lower_part


def per_device(columns, counts, nnz_count, selected):
    local_cells = columns.shape[0]
    row_slots = columns.shape[1]
    owners = lax.axis_size("gz")
    owner_index = lax.axis_index("gz")
    cells = local_cells * lax.axis_size("gx") * lax.axis_size("gy") * owners
    slot = lax.broadcasted_iota(jnp.int32, counts.shape, 1)
    live = slot < nnz_count[:, None]
    raw = jnp.where(live, counts.astype(jnp.float32), jnp.float32(0.0))
    library = jnp.sum(raw, axis=1, keepdims=True)
    values = jnp.log1p(raw * (target_sum / library))
    genes = jnp.where(live, columns, 0)
    block_rows = 4
    block_total = local_cells // block_rows
    expanded = lax.map(
        cell_block,
        (
            genes.reshape(block_total, block_rows, row_slots),
            values.reshape(block_total, block_rows, row_slots),
        ),
    )
    expanded = expanded.reshape(local_cells, GENES)
    total = jnp.sum(expanded, axis=0)
    square = jnp.sum(expanded * expanded, axis=0)
    terms = jnp.stack([total, square])
    owned = GENES // owners
    sums = lax.psum(terms, ("gx", "gy", "gz"))
    own_sums = lax.dynamic_slice_in_dim(sums, owner_index * owned, owned, 1)
    picked_sums = jnp.take(sums, selected, axis=1)
    own_mean = own_sums[0] / cells
    own_variance = own_sums[1] / cells - own_mean * own_mean
    gene_stats = jnp.stack([own_mean, own_variance])
    sel_mean = picked_sums[0] / cells
    sel_variance = picked_sums[1] / cells - sel_mean * sel_mean
    dense = jnp.take(expanded, selected, axis=1)
    share_size = SEL // owners
    own_mean_sel = lax.dynamic_slice_in_dim(sel_mean, owner_index * share_size, share_size, 0)
    own_variance_sel = lax.dynamic_slice_in_dim(
        sel_variance, owner_index * share_size, share_size, 0
    )
    moved = lax.all_to_all(
        dense.astype(jnp.bfloat16), "gz", split_axis=1, concat_axis=0, tiled=True
    ).astype(dense.dtype)
    pca_input = standardize(moved, own_mean_sel, own_variance_sel).astype(jnp.bfloat16)
    return (gene_stats, pca_input)


def solution(mesh):
    return jax.shard_map(
        per_device,
        mesh=mesh,
        in_specs=(
            P(("gx", "gy", "gz"), None),
            P(("gx", "gy", "gz"), None),
            P(("gx", "gy", "gz")),
            P(),
        ),
        out_specs=(P(None, "gz"), P(("gx", "gy"), "gz")),
        check_vma=False,
    )
```

profile of v0, /device:TPU:0, one launch (start us, length us, event | category | flops | bytes accessed | tf_op | source)
XLA Modules:
  0.0 230.8 jit_solution(16225255947262282294)
XLA Ops:
  7.2 0.0 all-reduce.2.cloned.1.call-start
  7.2 1.2 fusion.36
  8.4 1.1 multiply_log-plus-one_fusion
  9.5 0.1 reshape.103
  9.6 1.0 fusion.35
  10.7 0.1 reshape.102
  10.8 56.9 %while.12 = (s32[]{:T(128)}, f32[8,4,128,256]{3,2,1,0:T(8,128)}, s32[8,4,2048]{2,1,0:T(4,128)S(1)}, f32[8,4,2048]{2,1,0:T(4,128)S(1)}, s32[]{:T(128)}) while((s32[]{:T(128)}, f32[8,4,128,256]{3,2,1,0:T(8,128)}, s32[8,4,2048]{2,1,0:T(4,128)S(1)}, f32[8,4,2048]{2,1,0:T(4,128)S(1)}, s32[]{:T(128)}) %tuple.39), condition=%wide.region_2.3_spmd, body=%wide.region_1.2_spmd.sunk | while | flops 1084588032 | bytes 1982553 | solution.py:55
  10.8 0.1 add_select_fusion.4
  10.9 3.2 %fusion.48 = f32[4,128,256]{2,1,0:T(8,128)S(1)} fusion(s32[4,2048]{1,0:T(4,128)S(1)} %add_select_fusion.5, bf16[4,2048]{1,0:T(4,128)(2,1)S(1)} %bitcast_convert_fusion.2, s32[4,2048]{1,0:T(4,128)S(1)} %get-tuple-element.109), kind=kOutput, calls=%fused_computation.5.clone.1 | convolution fusion | flops 542113792 | bytes 606208 | tf_op jit(solution)/shard_map/while/body/eval_jaxpr/csh,csl->chl/dot_general | solution.py:32
  14.1 3.8 %fusion.50 = f32[8,4,128,256]{3,2,1,0:T(8,128)} fusion(f32[8,4,128,256]{3,2,1,0:T(8,128)} %get-tuple-element.116, s32[]{:T(128)S(6)} %copy.30, f32[4,128,256]{2,1,0:T(8,128)S(1)} %fusion.48, s32[4,2048]{1,0:T(4,128)S(1)} %add_select_fusion.5, bf16[4,2048]{1,0:T(4,128)(2,1)S(1)} %fusion.49, s32[4,2048]{1,0:T(4,128)S(1)} %get-tuple-element.109), kind=kOutput, calls=%fused_computation.18.clone.1 | convolution fusion | flops 542244864 | bytes 1130500 | tf_op jit(solution)/shard_map/while/body/eval_jaxpr/csh,csl->chl/dot_general | solution.py:35
  17.9 0.1 add_select_fusion.4
  18.0 3.2 %fusion.48 = f32[4,128,256]{2,1,0:T(8,128)S(1)} fusion(s32[4,2048]{1,0:T(4,128)S(1)} %add_select_fusion.5, bf16[4,2048]{1,0:T(4,128)(2,1)S(1)} %bitcast_convert_fusion.2, s32[4,2048]{1,0:T(4,128)S(1)} %get-tuple-element.109), kind=kOutput, calls=%fused_computation.5.clone.1 | convolution fusion | flops 542113792 | bytes 606208 | tf_op jit(solution)/shard_map/while/body/eval_jaxpr/csh,csl->chl/dot_general | solution.py:32
  21.2 3.8 %fusion.50 = f32[8,4,128,256]{3,2,1,0:T(8,128)} fusion(f32[8,4,128,256]{3,2,1,0:T(8,128)} %get-tuple-element.116, s32[]{:T(128)S(6)} %copy.30, f32[4,128,256]{2,1,0:T(8,128)S(1)} %fusion.48, s32[4,2048]{1,0:T(4,128)S(1)} %add_select_fusion.5, bf16[4,2048]{1,0:T(4,128)(2,1)S(1)} %fusion.49, s32[4,2048]{1,0:T(4,128)S(1)} %get-tuple-element.109), kind=kOutput, calls=%fused_computation.18.clone.1 | convolution fusion | flops 542244864 | bytes 1130500 | tf_op jit(solution)/shard_map/while/body/eval_jaxpr/csh,csl->chl/dot_general | solution.py:35
  25.0 0.1 add_select_fusion.4
  25.1 3.2 %fusion.48 = f32[4,128,256]{2,1,0:T(8,128)S(1)} fusion(s32[4,2048]{1,0:T(4,128)S(1)} %add_select_fusion.5, bf16[4,2048]{1,0:T(4,128)(2,1)S(1)} %bitcast_convert_fusion.2, s32[4,2048]{1,0:T(4,128)S(1)} %get-tuple-element.109), kind=kOutput, calls=%fused_computation.5.clone.1 | convolution fusion | flops 542113792 | bytes 606208 | tf_op jit(solution)/shard_map/while/body/eval_jaxpr/csh,csl->chl/dot_general | solution.py:32
  28.3 3.8 %fusion.50 = f32[8,4,128,256]{3,2,1,0:T(8,128)} fusion(f32[8,4,128,256]{3,2,1,0:T(8,128)} %get-tuple-element.116, s32[]{:T(128)S(6)} %copy.30, f32[4,128,256]{2,1,0:T(8,128)S(1)} %fusion.48, s32[4,2048]{1,0:T(4,128)S(1)} %add_select_fusion.5, bf16[4,2048]{1,0:T(4,128)(2,1)S(1)} %fusion.49, s32[4,2048]{1,0:T(4,128)S(1)} %get-tuple-element.109), kind=kOutput, calls=%fused_computation.18.clone.1 | convolution fusion | flops 542244864 | bytes 1130500 | tf_op jit(solution)/shard_map/while/body/eval_jaxpr/csh,csl->chl/dot_general | solution.py:35
  32.1 0.1 add_select_fusion.4
  32.3 3.2 %fusion.48 = f32[4,128,256]{2,1,0:T(8,128)S(1)} fusion(s32[4,2048]{1,0:T(4,128)S(1)} %add_select_fusion.5, bf16[4,2048]{1,0:T(4,128)(2,1)S(1)} %bitcast_convert_fusion.2, s32[4,2048]{1,0:T(4,128)S(1)} %get-tuple-element.109), kind=kOutput, calls=%fused_computation.5.clone.1 | convolution fusion | flops 542113792 | bytes 606208 | tf_op jit(solution)/shard_map/while/body/eval_jaxpr/csh,csl->chl/dot_general | solution.py:32
  35.4 3.8 %fusion.50 = f32[8,4,128,256]{3,2,1,0:T(8,128)} fusion(f32[8,4,128,256]{3,2,1,0:T(8,128)} %get-tuple-element.116, s32[]{:T(128)S(6)} %copy.30, f32[4,128,256]{2,1,0:T(8,128)S(1)} %fusion.48, s32[4,2048]{1,0:T(4,128)S(1)} %add_select_fusion.5, bf16[4,2048]{1,0:T(4,128)(2,1)S(1)} %fusion.49, s32[4,2048]{1,0:T(4,128)S(1)} %get-tuple-element.109), kind=kOutput, calls=%fused_computation.18.clone.1 | convolution fusion | flops 542244864 | bytes 1130500 | tf_op jit(solution)/shard_map/while/body/eval_jaxpr/csh,csl->chl/dot_general | solution.py:35
  39.3 0.1 add_select_fusion.4
  39.4 3.2 %fusion.48 = f32[4,128,256]{2,1,0:T(8,128)S(1)} fusion(s32[4,2048]{1,0:T(4,128)S(1)} %add_select_fusion.5, bf16[4,2048]{1,0:T(4,128)(2,1)S(1)} %bitcast_convert_fusion.2, s32[4,2048]{1,0:T(4,128)S(1)} %get-tuple-element.109), kind=kOutput, calls=%fused_computation.5.clone.1 | convolution fusion | flops 542113792 | bytes 606208 | tf_op jit(solution)/shard_map/while/body/eval_jaxpr/csh,csl->chl/dot_general | solution.py:32
  42.5 3.8 %fusion.50 = f32[8,4,128,256]{3,2,1,0:T(8,128)} fusion(f32[8,4,128,256]{3,2,1,0:T(8,128)} %get-tuple-element.116, s32[]{:T(128)S(6)} %copy.30, f32[4,128,256]{2,1,0:T(8,128)S(1)} %fusion.48, s32[4,2048]{1,0:T(4,128)S(1)} %add_select_fusion.5, bf16[4,2048]{1,0:T(4,128)(2,1)S(1)} %fusion.49, s32[4,2048]{1,0:T(4,128)S(1)} %get-tuple-element.109), kind=kOutput, calls=%fused_computation.18.clone.1 | convolution fusion | flops 542244864 | bytes 1130500 | tf_op jit(solution)/shard_map/while/body/eval_jaxpr/csh,csl->chl/dot_general | solution.py:35
  46.4 0.1 add_select_fusion.4
  46.5 3.2 %fusion.48 = f32[4,128,256]{2,1,0:T(8,128)S(1)} fusion(s32[4,2048]{1,0:T(4,128)S(1)} %add_select_fusion.5, bf16[4,2048]{1,0:T(4,128)(2,1)S(1)} %bitcast_convert_fusion.2, s32[4,2048]{1,0:T(4,128)S(1)} %get-tuple-element.109), kind=kOutput, calls=%fused_computation.5.clone.1 | convolution fusion | flops 542113792 | bytes 606208 | tf_op jit(solution)/shard_map/while/body/eval_jaxpr/csh,csl->chl/dot_general | solution.py:32
  49.6 3.8 %fusion.50 = f32[8,4,128,256]{3,2,1,0:T(8,128)} fusion(f32[8,4,128,256]{3,2,1,0:T(8,128)} %get-tuple-element.116, s32[]{:T(128)S(6)} %copy.30, f32[4,128,256]{2,1,0:T(8,128)S(1)} %fusion.48, s32[4,2048]{1,0:T(4,128)S(1)} %add_select_fusion.5, bf16[4,2048]{1,0:T(4,128)(2,1)S(1)} %fusion.49, s32[4,2048]{1,0:T(4,128)S(1)} %get-tuple-element.109), kind=kOutput, calls=%fused_computation.18.clone.1 | convolution fusion | flops 542244864 | bytes 1130500 | tf_op jit(solution)/shard_map/while/body/eval_jaxpr/csh,csl->chl/dot_general | solution.py:35
  53.5 0.1 add_select_fusion.4
  53.6 3.2 %fusion.48 = f32[4,128,256]{2,1,0:T(8,128)S(1)} fusion(s32[4,2048]{1,0:T(4,128)S(1)} %add_select_fusion.5, bf16[4,2048]{1,0:T(4,128)(2,1)S(1)} %bitcast_convert_fusion.2, s32[4,2048]{1,0:T(4,128)S(1)} %get-tuple-element.109), kind=kOutput, calls=%fused_computation.5.clone.1 | convolution fusion | flops 542113792 | bytes 606208 | tf_op jit(solution)/shard_map/while/body/eval_jaxpr/csh,csl->chl/dot_general | solution.py:32
  56.7 3.8 %fusion.50 = f32[8,4,128,256]{3,2,1,0:T(8,128)} fusion(f32[8,4,128,256]{3,2,1,0:T(8,128)} %get-tuple-element.116, s32[]{:T(128)S(6)} %copy.30, f32[4,128,256]{2,1,0:T(8,128)S(1)} %fusion.48, s32[4,2048]{1,0:T(4,128)S(1)} %add_select_fusion.5, bf16[4,2048]{1,0:T(4,128)(2,1)S(1)} %fusion.49, s32[4,2048]{1,0:T(4,128)S(1)} %get-tuple-element.109), kind=kOutput, calls=%fused_computation.18.clone.1 | convolution fusion | flops 542244864 | bytes 1130500 | tf_op jit(solution)/shard_map/while/body/eval_jaxpr/csh,csl->chl/dot_general | solution.py:35
  60.6 0.1 add_select_fusion.4
  60.7 3.2 %fusion.48 = f32[4,128,256]{2,1,0:T(8,128)S(1)} fusion(s32[4,2048]{1,0:T(4,128)S(1)} %add_select_fusion.5, bf16[4,2048]{1,0:T(4,128)(2,1)S(1)} %bitcast_convert_fusion.2, s32[4,2048]{1,0:T(4,128)S(1)} %get-tuple-element.109), kind=kOutput, calls=%fused_computation.5.clone.1 | convolution fusion | flops 542113792 | bytes 606208 | tf_op jit(solution)/shard_map/while/body/eval_jaxpr/csh,csl->chl/dot_general | solution.py:32
  63.8 3.8 %fusion.50 = f32[8,4,128,256]{3,2,1,0:T(8,128)} fusion(f32[8,4,128,256]{3,2,1,0:T(8,128)} %get-tuple-element.116, s32[]{:T(128)S(6)} %copy.30, f32[4,128,256]{2,1,0:T(8,128)S(1)} %fusion.48, s32[4,2048]{1,0:T(4,128)S(1)} %add_select_fusion.5, bf16[4,2048]{1,0:T(4,128)(2,1)S(1)} %fusion.49, s32[4,2048]{1,0:T(4,128)S(1)} %get-tuple-element.109), kind=kOutput, calls=%fused_computation.18.clone.1 | convolution fusion | flops 542244864 | bytes 1130500 | tf_op jit(solution)/shard_map/while/body/eval_jaxpr/csh,csl->chl/dot_general | solution.py:35
  67.7 0.0 copy-start.1
  67.7 2.6 %fusion.39 = (f32[128,256]{1,0:T(8,128)S(1)}, f32[128,256]{1,0:T(8,128)S(1)}) fusion(f32[8,4,128,256]{3,2,1,0:T(8,128)} %get-tuple-element.58), kind=kLoop, calls=%fused_computation.62 | loop fusion | flops 3080192 | bytes 4456448 | tf_op jit(solution)/shard_map/reduce_sum | solution.py:63
  70.3 0.1 copy.24
  70.4 0.1 copy.25
  70.6 0.9 pad_maximum_fusion
  71.5 0.0 all-reduce.2.cloned.1.call-update
  71.6 0.0 copy-done.1
  71.6 4.4 %copy.26 = bf16[4,8,128,256]{3,1,2,0:T(8,128)(2,1)S(1)} copy(f32[4,8,128,256]{3,2,1,0:T(8,128)} %bitcast.62) | data formatting | bytes 6291456
  76.0 6.0 %copy.21 = bf16[32,32768]{0,1:T(8,128)(2,1)} copy(bf16[32,32768]{1,0:T(8,128)(2,1)S(1)} %bitcast.63) | data formatting | bytes 4194304 | tf_op jit(solution)/shard_map/reshape | solution.py:62
  82.0 10.1 %gather_fusion = bf16[2048,32]{1,0:T(8,128)(2,1)S(1)} fusion(bf16[32,32768]{0,1:T(8,128)(2,1)} %copy.21, s32[2048]{0:T(1024)S(1)} %fusion.38), kind=kCustom, calls=%fused_computation | custom fusion | bytes 270336 | tf_op jit(solution)/shard_map/jit(_take)/gather | solution.py:75
  92.1 0.2 copy.22
  92.3 0.7 select_convert_fusion
  93.0 4.3 %all-to-all-start = ((bf16[32,2,1024]{2,0,1:T(8,128)(2,1)}), bf16[32,2,1024]{2,0,1:T(8,128)(2,1)S(1)}, u32[]{:S(2)}, u32[]{:S(2)}) async-start(bf16[32,2,1024]{2,0,1:T(8,128)(2,1)} %select_convert_fusion), calls=%async_computation | async-start | bytes 262144 | tf_op jit(solution)/shard_map/all_to_all | solution.py:81
  97.3 103.7 %all-reduce.2.cloned.1.call-done = f32[2,32768]{1,0:T(2,128)} async-done(((f32[2,32768]{1,0:T(2,128)}), f32[2,32768]{1,0:T(2,128)}) %all-reduce.2.cloned.1.call-update) | async-done | bytes 262160 | tf_op jit(solution)/shard_map/psum | solution.py:67
  201.0 0.0 copy-start
  201.0 8.9 %copy.23 = f32[2,32768]{0,1:T(8,128)} copy(f32[2,32768]{1,0:T(2,128)} %all-reduce.2.cloned.1.call-done) | data formatting | bytes 524288 | tf_op jit(solution)/shard_map/psum | solution.py:67
  209.9 11.2 %gather_fusion.1 = f32[2048,2]{1,0:T(8,128)S(1)} fusion(f32[2,32768]{0,1:T(8,128)} %copy.23, s32[2048]{0:T(1024)S(1)} %fusion.38), kind=kCustom, calls=%fused_computation.1 | custom fusion | bytes 40960 | tf_op jit(solution)/shard_map/jit(_take)/gather | solution.py:69
  221.2 0.3 select_bitcast_fusion
  221.5 0.0 copy-done
  221.5 0.2 dynamic-slice_multiply_fusion.2
  221.7 0.8 pad_maximum_fusion.1
  222.5 0.3 fusion.40
  222.9 0.4 dynamic-slice_reduce_fusion
  223.2 0.0 all-to-all-done
  223.2 0.7 fusion.34
  (29 shorter events, 0.5 us)
Async XLA Ops:
  7.2 193.8 %all-reduce.2.cloned.1.call-start = ((), (), s32[]{:S(2)}) async-start(), calls=%async_computation.1 | async-start | bytes 524288 | tf_op jit(solution)/shard_map/psum | solution.py:67
  67.7 3.9 %copy-start.1 = (s32[2048]{0:T(1024)S(1)}, s32[2048]{0:T(1024)}, u32[]{:S(2)}) copy-start(s32[2048]{0:T(1024)} %param.9) | copy-start | bytes 24580
  93.0 130.2 %all-to-all-start = ((bf16[32,2,1024]{2,0,1:T(8,128)(2,1)}), bf16[32,2,1024]{2,0,1:T(8,128)(2,1)S(1)}, u32[]{:S(2)}, u32[]{:S(2)}) async-start(bf16[32,2,1024]{2,0,1:T(8,128)(2,1)} %select_convert_fusion), calls=%async_computation | async-start | bytes 262144 | tf_op jit(solution)/shard_map/all_to_all | solution.py:81
  201.0 20.5 %copy-start = (f32[2,32768]{1,0:T(2,128)S(1)}, f32[2,32768]{1,0:T(2,128)}, u32[]{:S(2)}) copy-start(f32[2,32768]{1,0:T(2,128)} %all-reduce.2.cloned.1.call-done) | copy-start | bytes 786436
Sparse Core Ops, SparseCore 0:
  71.7 129.2 all-reduce.1
where the time goes:
time: 231 us
  waiting for transfers between devices  104 us (45%)
  matrix products  55.7 us (24%)
  local copies, waits for them, and re-layouts  41.3 us (18%)
  between operations  14.2 us (6%)
  other arithmetic  11.3 us (5%)
  starting transfers between devices  4.31 us (2%)
    psum x1, waiting for transfers between devices, per_device(): sums = lax.psum(terms, ('gx', 'gy', 'gz'))  104 us
    dot_general x8, matrix products, cell_block(): jnp.einsum('csh,csl->chl', high_table, lower_table, preferred_element_typ...  30.5 us
    dot_general x8, matrix products, cell_block(): jnp.einsum('csh,csl->chl', high_table, upper_table, preferred_element_typ...  25.2 us
    gather x1, local copies, waits for them, and re-layouts, per_device(): picked_sums = jnp.take(sums, selected, axis=1)  11.2 us
    gather x2, local copies, waits for them, and re-layouts, per_device(): dense = jnp.take(expanded, selected, axis=1)  10.3 us
    psum x1, local copies, waits for them, and re-layouts, per_device(): sums = lax.psum(terms, ('gx', 'gy', 'gz'))  8.92 us
    reshape x1, local copies, waits for them, and re-layouts, per_device(): expanded = expanded.reshape(local_cells, GENES)  5.99 us
    unnamed x7, local copies, waits for them, and re-layouts  4.7 us
  transfers between devices with their start and end apart: 2, of which 1 were waited for; matrix products, arithmetic and copies ran while one was open for 19% of the time, Pallas kernels for 0%

commit v1 on v0

v1 whole, which is shorter than its diff:
```python
import functools

import jax
import jax.numpy as jnp
from jax import lax
from jax.experimental import pallas as pl
from jax.experimental.pallas import tpu as pltpu
from jax.sharding import PartitionSpec as P

GENES = 32768
STRIDE = 16
LANES = 128
HIGH = GENES // (STRIDE * LANES)

target_sum = 10000.0
var_floor = 0.01
clip_value = 10.0

f32 = jnp.float32
bf16 = jnp.bfloat16


def tile_of_rows(ref, row, start, width):
    return jnp.broadcast_to(ref[pl.ds(row, 1), pl.ds(start, width)], (16, width)).astype(bf16)


def one_hot_lanes(low16, ids, width):
    groups = []
    for g in range(LANES // 16):
        hit = low16 == (ids + bf16(16.0 * g))
        groups.append(jnp.where(hit, bf16(1.0), bf16(0.0)))
    return groups


def scatter_kernel(owner_ref, columns_ref, counts_ref, nnz_ref, *refs, owners):
    compact_ref, scale_ref = refs[0], refs[1]
    total_refs = refs[2:2 + owners]
    low_s, high_s, off_s, count_s, total_s = refs[2 + owners:]
    rows, slots = columns_ref.shape
    i0 = lax.broadcasted_iota(jnp.int32, (rows, rows), 0)
    i1 = lax.broadcasted_iota(jnp.int32, (rows, rows), 1)
    nnz = jnp.broadcast_to(nnz_ref[...].astype(f32), (rows, rows))
    nnz = jnp.sum(jnp.where(i0 == i1, nnz, f32(0.0)), axis=1, keepdims=True).astype(jnp.int32)
    live = lax.broadcasted_iota(jnp.int32, (rows, slots), 1) < nnz
    columns = columns_ref[...]
    count = jnp.where(live, counts_ref[...], 0).astype(f32)
    count_s[...] = count
    low_s[...] = ((columns // STRIDE) % LANES).astype(f32)
    high_s[...] = jnp.where(live, columns // (STRIDE * LANES), -1).astype(f32)
    off_s[...] = (columns % STRIDE).astype(f32)
    library = jnp.sum(count, axis=1, keepdims=True)
    scale_ref[...] = jnp.broadcast_to(target_sum / library, (rows, LANES))
    width = min(256, slots)
    ids = lax.broadcasted_iota(jnp.int32, (16, width), 0).astype(f32).astype(bf16)

    def one_cell(c):
        acc = jnp.zeros((2 * HIGH, LANES), f32)
        for start in range(0, slots, width):
            low16 = tile_of_rows(low_s, c, start, width)
            high16 = tile_of_rows(high_s, c, start, width)
            off16 = tile_of_rows(off_s, c, start, width)
            count16 = tile_of_rows(count_s, c, start, width)
            table = jnp.concatenate(one_hot_lanes(low16, ids, width), axis=0)
            hit = high16 == ids
            payload = jnp.concatenate(
                [jnp.where(hit, off16, bf16(0.0)), jnp.where(hit, count16, bf16(0.0))], axis=0
            )
            acc = acc + lax.dot_general(
                payload, table, (((1,), (1,)), ((), ())), preferred_element_type=f32
            )
        base = pl.multiple_of(c * 2 * HIGH, 2 * HIGH)
        compact_ref[pl.ds(base, HIGH), :] = acc[:HIGH]
        compact_ref[pl.ds(base + HIGH, HIGH), :] = jnp.log(
            f32(1.0) + acc[HIGH:] * scale_ref[pl.ds(c, 1), :]
        )

    def cells(step, carry):
        for u in range(4):
            one_cell(step * 4 + u)
        return carry

    lax.fori_loop(0, rows // 4, cells, 0)

    def offsets(o, carry):
        o_f = o.astype(f32)
        total = jnp.zeros((HIGH, LANES), f32)
        square = jnp.zeros((HIGH, LANES), f32)
        for c in range(rows):
            off = compact_ref[pl.ds(c * 2 * HIGH, HIGH), :]
            value = compact_ref[pl.ds(c * 2 * HIGH + HIGH, HIGH), :]
            value = jnp.where(off == o_f, value, f32(0.0))
            total = total + value
            square = square + value * value
        total_s[0] = total
        total_s[1] = square
        own_high = HIGH // owners
        for d in range(owners):
            start = lax.rem(owner_ref[0] + d, owners) * own_high
            for s in range(2):
                total_refs[d][pl.ds((o * 2 + s) * own_high, own_high), :] = total_s[
                    s, pl.ds(start, own_high), :
                ]
        return carry

    lax.fori_loop(0, STRIDE, offsets, 0)


def select_kernel(owner_ref, compact_ref, scale_ref, selected_ref, *refs, owners):
    dense_refs = refs[:owners]
    sum_refs = refs[owners:2 * owners]
    pairs_s = refs[2 * owners]
    rows = scale_ref.shape[0]
    share = selected_ref.shape[1]
    width = min(256, share)
    for h in range(HIGH):
        lanes = pl.ds((h % 2) * LANES, LANES)
        pairs_s[h // 2, pl.ds(0, rows), lanes] = compact_ref[
            pl.ds(h, rows, stride=2 * HIGH), :
        ].astype(bf16)
        value = compact_ref[pl.ds(HIGH + h, rows, stride=2 * HIGH), :]
        upper = value.astype(bf16)
        pairs_s[h // 2, pl.ds(rows, rows), lanes] = upper
        pairs_s[h // 2, pl.ds(2 * rows, rows), lanes] = (value - upper.astype(f32)).astype(bf16)
    ids = lax.broadcasted_iota(jnp.int32, (16, width), 0).astype(f32).astype(bf16)
    for d in range(owners):
        owner = lax.rem(owner_ref[0] + d, owners)
        for start in range(0, share, width):
            picked = selected_ref[pl.ds(owner, 1), pl.ds(start, width)]
            low16 = jnp.broadcast_to(
                ((picked // STRIDE) % LANES).astype(f32), (16, width)
            ).astype(bf16)
            high16 = jnp.broadcast_to(
                (picked // (STRIDE * LANES)).astype(f32), (16, width)
            ).astype(bf16)
            low_hot = one_hot_lanes(low16, ids, width)
            acc = jnp.zeros((3 * rows, width), f32)
            for pair in range(HIGH // 2):
                parts = []
                for h in (2 * pair, 2 * pair + 1):
                    hit = high16 == bf16(float(h))
                    parts += [jnp.where(hit, part, bf16(0.0)) for part in low_hot]
                acc = acc + jnp.dot(
                    pairs_s[pair], jnp.concatenate(parts, axis=0), preferred_element_type=f32
                )
            off = (picked % STRIDE).astype(f32)
            value = acc[rows:2 * rows] + acc[2 * rows:]
            dense = jnp.where(acc[:rows] == off, value, f32(0.0))
            dense_refs[d][:, pl.ds(start, width)] = dense.astype(dense_refs[d].dtype)
            sum_refs[d][pl.ds(0, 1), pl.ds(start, width)] = jnp.sum(dense, axis=0, keepdims=True)
            sum_refs[d][pl.ds(1, 1), pl.ds(start, width)] = jnp.sum(
                dense * dense, axis=0, keepdims=True
            )


def shift(value, axis, d):
    n = lax.axis_size(axis)
    return lax.ppermute(value, axis, [(s, (s + d) % n) for s in range(n)])


def per_device(columns, counts, nnz_count, selected):
    rows, slots = columns.shape
    sel = selected.shape[0]
    owners = lax.axis_size("gz")
    outer = lax.axis_size("gx")
    middle = lax.axis_size("gy")
    cells = rows * outer * middle * owners
    owner = lax.axis_index("gz")
    place = lax.axis_index("gx")
    share = sel // owners
    own_high = HIGH // owners
    sum_rows = STRIDE * 2 * own_high
    vmem = pl.BlockSpec(memory_space=pltpu.VMEM)
    smem = pl.BlockSpec(memory_space=pltpu.SMEM)
    owner_arg = owner.reshape(1).astype(jnp.int32)

    made = pl.pallas_call(
        functools.partial(scatter_kernel, owners=owners),
        out_shape=[
            jax.ShapeDtypeStruct((rows * 2 * HIGH, LANES), f32),
            jax.ShapeDtypeStruct((rows, LANES), f32),
        ] + [jax.ShapeDtypeStruct((sum_rows, LANES), f32)] * owners,
        in_specs=[smem, vmem, vmem, vmem],
        out_specs=[vmem] * (2 + owners),
        scratch_shapes=[pltpu.VMEM((rows, slots), f32)] * 4 + [pltpu.VMEM((2, HIGH, LANES), f32)],
        name="scatter",
    )(owner_arg, columns, counts, nnz_count.reshape(1, rows))
    compact, scale, sums = made[0], made[1], made[2:]
    moved_sums = [shift(sums[d], "gz", d) for d in range(1, owners)]

    picked = pl.pallas_call(
        functools.partial(select_kernel, owners=owners),
        out_shape=[jax.ShapeDtypeStruct((rows, share), f32)]
        + [jax.ShapeDtypeStruct((rows, share), bf16)] * (owners - 1)
        + [jax.ShapeDtypeStruct((2, share), f32)] * owners,
        in_specs=[smem, vmem, vmem, vmem],
        out_specs=[vmem] * (2 * owners),
        scratch_shapes=[pltpu.VMEM((HIGH // 2, 3 * rows, 2 * LANES), bf16)],
        name="select",
    )(owner_arg, compact, scale, selected.reshape(owners, share))
    dense, picked_sums = picked[:owners], picked[owners:]
    moved_picked = [shift(picked_sums[d], "gz", d) for d in range(1, owners)]
    moved_dense = [shift(dense[d], "gz", d) for d in range(1, owners)]

    gene_sums = functools.reduce(jnp.add, [sums[0]] + moved_sums)
    sel_sums = functools.reduce(jnp.add, [picked_sums[0]] + moved_picked)
    chunk_rows = sum_rows // outer
    sel_part = sel_sums.reshape(2, outer, share // outer).transpose(1, 0, 2).reshape(outer, -1)
    extra = -(-sel_part.shape[1] // (8 * LANES)) * 8
    sel_part = jnp.pad(sel_part, ((0, 0), (0, extra * LANES - sel_part.shape[1])))
    both = jnp.concatenate(
        [gene_sums.reshape(outer, chunk_rows, LANES), sel_part.reshape(outer, extra, LANES)], axis=1
    )

    def chunk(index):
        return lax.dynamic_index_in_dim(both, index, 0, keepdims=False)

    part = functools.reduce(
        jnp.add,
        [chunk(place)] + [shift(chunk(lax.rem(place + d, outer)), "gx", d) for d in range(1, outer)],
    )
    part = functools.reduce(jnp.add, [part] + [shift(part, "gy", d) for d in range(1, middle)])
    held = jnp.stack([part] + [shift(part, "gx", d) for d in range(1, outer)])
    full = jnp.stack(
        [
            lax.dynamic_index_in_dim(held, lax.rem(place + outer - i, outer), 0, keepdims=False)
            for i in range(outer)
        ]
    )
    genes = full[:, :chunk_rows].reshape(STRIDE, 2, own_high * LANES)
    mean = genes[:, 0] / cells
    variance = genes[:, 1] / cells - mean * mean
    gene_stats = jnp.stack([mean, variance]).transpose(0, 2, 1).reshape(2, -1)
    part_size = share // outer
    sel_full = full[:, chunk_rows:].reshape(outer, -1)[:, :2 * part_size]
    sel_full = sel_full.reshape(outer, 2, part_size).transpose(1, 0, 2).reshape(2, share)
    sel_mean = sel_full[0] / cells
    sel_variance = sel_full[1] / cells - sel_mean * sel_mean
    sel_scale = jnp.sqrt(jnp.maximum(sel_variance, var_floor))
    blocks = jnp.stack([dense[0]] + [m.astype(f32) for m in moved_dense])
    ordered = jnp.concatenate(
        [
            lax.dynamic_index_in_dim(blocks, lax.rem(owner + owners - q, owners), 0, keepdims=False)
            for q in range(owners)
        ],
        axis=0,
    )
    pca_input = jnp.clip((ordered - sel_mean) / sel_scale, -clip_value, clip_value).astype(bf16)
    return (gene_stats, pca_input)


def solution(mesh):
    return jax.shard_map(
        per_device,
        mesh=mesh,
        in_specs=(
            P(("gx", "gy", "gz"), None),
            P(("gx", "gy", "gz"), None),
            P(("gx", "gy", "gz")),
            P(),
        ),
        out_specs=(P(None, "gz"), P(("gx", "gy"), "gz")),
        check_vma=False,
    )
```

time: 231 us -> 44.6 us (0.19)
  waiting for transfers between devices: 104 us -> 13.3 us
  matrix products: 55.7 us -> 0 us
  local copies, waits for them, and re-layouts: 41.3 us -> 2.36 us
  between operations: 14.2 us -> 0.83 us
  Pallas kernels: 0 us -> 13.3 us
  other arithmetic: 11.3 us -> 1.87 us
  starting transfers between devices: 4.31 us -> 12.7 us
    psum x1 -> x0, waiting for transfers between devices: 104 us -> none  [per_device(): sums = lax.psum(terms, ('gx', 'gy', 'gz'))]
    dot_general x16 -> x0, matrix products: 55.7 us -> none  [the longest x8 30.5 us: cell_block(): jnp.einsum('csh,csl->chl', high_table, lower_table, preferred_element_typ...]
    gather x3 -> x0, local copies, waits for them, and re-layouts: 21.5 us -> none  [the longest x1 11.2 us: per_device(): picked_sums = jnp.take(sums, selected, axis=1)]
    pallas_call x0 -> x2, Pallas kernels: none -> 13.3 us  [the longest x1 9.88 us: per_device(): pl.pallas_call(functools.partial(scatter_kernel, owners=owners), out_shap...]
    ppermute x0 -> x12, waiting for transfers between devices: none -> 13.3 us  [shift(): return lax.ppermute(value, axis, [(s, (s + d) % n) for s in range(n)])]
    ppermute x0 -> x12, starting transfers between devices: none -> 12.7 us  [shift(): return lax.ppermute(value, axis, [(s, (s + d) % n) for s in range(n)])]
    psum x1 -> x0, local copies, waits for them, and re-layouts: 8.92 us -> none  [per_device(): sums = lax.psum(terms, ('gx', 'gy', 'gz'))]
    unnamed x7 -> x11, local copies, waits for them, and re-layouts: 4.7 us -> 0.03 us
  transfers between devices with their start and end apart: 2 -> 12, of which waited for: 1 -> 8; matrix products, arithmetic and copies ran while one was open for 19% -> 3% of each run, Pallas kernels for 0% -> 8%
where the time goes in v1:
time: 44.6 us; the launch traced here: 44.4 us
  Pallas kernels  13.3 us (30%)
  waiting for transfers between devices  13.3 us (30%)
  starting transfers between devices  12.7 us (28%)
  local copies, waits for them, and re-layouts  2.36 us (5%)
  other arithmetic  1.87 us (4%)
  between operations  0.83 us (2%)
    ppermute x12, waiting for transfers between devices, shift(): return lax.ppermute(value, axis, [(s, (s + d) % n) for s in range(n)])  13.3 us
    ppermute x12, starting transfers between devices, shift(): return lax.ppermute(value, axis, [(s, (s + d) % n) for s in range(n)])  12.7 us
    pallas_call x1, Pallas kernels, per_device(): pl.pallas_call(functools.partial(scatter_kernel, owners=owners), out_shap...  9.88 us
    pallas_call x1, Pallas kernels, per_device(): pl.pallas_call(functools.partial(select_kernel, owners=owners), out_shape...  3.43 us
    reshape x1, local copies, waits for them, and re-layouts, per_device(): gene_stats = jnp.stack([mean, variance]).transpose(0, 2, 1).reshape(2, -1)  1.23 us
  transfers between devices with their start and end apart: 12, of which 8 were waited for; matrix products, arithmetic and copies ran while one was open for 3% of the time, Pallas kernels for 8%

profile of v1, /device:TPU:0, one launch (start us, length us, event | category | flops | bytes accessed | tf_op | source)
XLA Modules:
  0.0 44.4 jit_solution(11164288571401336089)
XLA Ops:
  0.6 0.0 copy-start.2
  0.6 9.9 %scatter.1 = (f32[1024,128]{1,0:T(8,128)}, f32[32,128]{1,0:T(8,128)}, f32[256,128]{1,0:T(8,128)}, f32[256,128]{1,0:T(8,128)}) custom-call(s32[1]{0:T(128)} %bitcast.owner_ref, s32[32,2048]{1,0:T(8,128)} %columns_ref.1, s32[32,2048]{1,0:T(8,128)} %counts_ref.1, s32[1,32]{1,0:T(1,128)} %bitcast.70), custom_call_target="tpu_custom_call" | custom-call | tf_op jit(solution)/shard_map/scatter/pallas_call | solution.py:176
  10.5 3.0 %collective-permute-start = (f32[256,128]{1,0:T(8,128)}, f32[256,128]{1,0:T(8,128)S(1)}, u32[]{:S(2)}, u32[]{:S(2)}) collective-permute-start(f32[256,128]{1,0:T(8,128)} %get-tuple-element.11), channel_id=1, source_target_pairs={{0,1},{1,0},{2,3},{3,2},{4,5},{5,4},{6,7},{7,6},{8,9},{9,8},{10,11... | collective-permute-start | bytes 393224 | tf_op jit(solution)/shard_map/ppermute | solution.py:157
  13.5 0.0 copy-done.2
  13.5 0.6 %reshape.100.selected_ref = s32[2,1024]{1,0:T(2,128)} reshape(s32[2048]{0:T(1024)S(1)} %copy-done.2) | data formatting | bytes 16384 | tf_op jit(solution)/shard_map/reshape | solution.py:199
  14.1 3.4 %select.20 = (f32[32,1024]{1,0:T(8,128)}, bf16[32,1024]{1,0:T(8,128)(2,1)}, f32[2,1024]{1,0:T(2,128)}, f32[2,1024]{1,0:T(2,128)}) custom-call(s32[1]{0:T(128)} %bitcast.owner_ref, f32[1024,128]{1,0:T(8,128)} %get-tuple-element.12.compact_ref, f32[32,128]{1,0:T(8,128)} %get-tuple-element.13.scale_ref, s32[2,1024]{1,0:T(2,128)} %reshape.100.selected_ref), custom_call_target="tpu_custom_call" | custom-call | tf_op jit(solution)/shard_map/select/pallas_call | solution.py:190
  17.6 0.0 copy-start
  17.6 0.0 collective-permute-start.1
  17.6 3.8 %collective-permute-done.1 = f32[2,1024]{1,0:T(2,128)S(1)} collective-permute-done((f32[2,1024]{1,0:T(2,128)}, f32[2,1024]{1,0:T(2,128)S(1)}, u32[]{:S(2)}, u32[]{:S(2)}) %collective-permute-start.1) | collective-permute-done | bytes 8224 | tf_op jit(solution)/shard_map/ppermute | solution.py:157
  21.4 0.7 %add.82 = f32[2,1024]{1,0:T(2,128)S(1)} add(f32[2,1024]{1,0:T(2,128)} %get-tuple-element.14, f32[2,1024]{1,0:T(2,128)S(1)} %collective-permute-done.1) | non-fusion elementwise | flops 2048 | bytes 24576 | tf_op jit(solution)/shard_map/add | solution.py:205
  22.2 0.0 collective-permute-done
  22.2 0.0 copy-done
  22.2 0.0 copy-start.3
  22.2 0.1 collective-permute-start.2
  22.3 1.6 %collective-permute-start.3 = (f32[72,128]{1,0:T(8,128)S(1)}, f32[72,128]{1,0:T(8,128)S(1)}, u32[]{:S(2)}, u32[]{:S(2)}) collective-permute-start(f32[72,128]{1,0:T(8,128)S(1)} %get-tuple-element.25), channel_id=1, source_target_pairs={{0,16},{8,24},{16,0},{24,8},{1,17},{9,25},{17,1},{25,9},{2,18},{10... | collective-permute-start | bytes 110600 | tf_op jit(solution)/shard_map/ppermute | solution.py:157
  23.9 1.4 %collective-permute-start.4 = (f32[72,128]{1,0:T(8,128)S(1)}, f32[72,128]{1,0:T(8,128)S(1)}, u32[]{:S(2)}, u32[]{:S(2)}) collective-permute-start(f32[72,128]{1,0:T(8,128)S(1)} %get-tuple-element.26), channel_id=1, source_target_pairs={{0,24},{8,0},{16,8},{24,16},{1,25},{9,1},{17,9},{25,17},{2,26},{10... | collective-permute-start | bytes 110600 | tf_op jit(solution)/shard_map/ppermute | solution.py:157
  25.3 0.0 copy-done.3
  25.3 0.5 %collective-permute-start.11 = (bf16[32,1024]{1,0:T(8,128)(2,1)S(1)}, bf16[32,1024]{1,0:T(8,128)(2,1)S(1)}, u32[]{:S(2)}, u32[]{:S(2)}) collective-permute-start(bf16[32,1024]{1,0:T(8,128)(2,1)S(1)} %copy-done.3), channel_id=1, source_target_pairs={{0,1},{1,0},{2,3},{3,2},{4,5},{5,4},{6,7},{7,6},{8,9},{9,8},{10,11... | collective-permute-start | bytes 196616 | tf_op jit(solution)/shard_map/ppermute | solution.py:157
  25.8 0.0 collective-permute-done.2
  25.8 0.6 %collective-permute-done.3 = f32[72,128]{1,0:T(8,128)S(1)} collective-permute-done((f32[72,128]{1,0:T(8,128)S(1)}, f32[72,128]{1,0:T(8,128)S(1)}, u32[]{:S(2)}, u32[]{:S(2)}) %collective-permute-start.3) | collective-permute-done | bytes 36896 | tf_op jit(solution)/shard_map/ppermute | solution.py:157
  26.3 0.6 %collective-permute-done.4 = f32[72,128]{1,0:T(8,128)S(1)} collective-permute-done((f32[72,128]{1,0:T(8,128)S(1)}, f32[72,128]{1,0:T(8,128)S(1)}, u32[]{:S(2)}, u32[]{:S(2)}) %collective-permute-start.4) | collective-permute-done | bytes 36896 | tf_op jit(solution)/shard_map/ppermute | solution.py:157
  26.9 3.7 %collective-permute-start.7 = (f32[72,128]{1,0:T(8,128)S(1)}, f32[72,128]{1,0:T(8,128)S(1)}, u32[]{:S(2)}, u32[]{:S(2)}) collective-permute-start(f32[72,128]{1,0:T(8,128)S(1)} %fusion.16), channel_id=1, source_target_pairs={{0,6},{2,0},{4,2},{6,4},{1,7},{3,1},{5,3},{7,5},{8,14},{10,8},{12,... | collective-permute-start | bytes 110600 | tf_op jit(solution)/shard_map/ppermute | solution.py:157
  30.6 0.0 collective-permute-start.6
  30.6 1.0 %collective-permute-start.5 = (f32[72,128]{1,0:T(8,128)S(1)}, f32[72,128]{1,0:T(8,128)S(1)}, u32[]{:S(2)}, u32[]{:S(2)}) collective-permute-start(f32[72,128]{1,0:T(8,128)S(1)} %fusion.16), channel_id=1, source_target_pairs={{0,2},{2,4},{4,6},{6,0},{1,3},{3,5},{5,7},{7,1},{8,10},{10,12},{12... | collective-permute-start | bytes 110600 | tf_op jit(solution)/shard_map/ppermute | solution.py:157
  31.6 0.0 collective-permute-done.11
  31.6 0.0 copy-start.1
  31.6 0.9 %collective-permute-done.7 = f32[72,128]{1,0:T(8,128)S(1)} collective-permute-done((f32[72,128]{1,0:T(8,128)S(1)}, f32[72,128]{1,0:T(8,128)S(1)}, u32[]{:S(2)}, u32[]{:S(2)}) %collective-permute-start.7) | collective-permute-done | bytes 36896 | tf_op jit(solution)/shard_map/ppermute | solution.py:157
  32.5 3.0 %collective-permute-done.6 = f32[72,128]{1,0:T(8,128)S(1)} collective-permute-done((f32[72,128]{1,0:T(8,128)S(1)}, f32[72,128]{1,0:T(8,128)S(1)}, u32[]{:S(2)}, u32[]{:S(2)}) %collective-permute-start.6) | collective-permute-done | bytes 36896 | tf_op jit(solution)/shard_map/ppermute | solution.py:157
  35.4 0.9 %collective-permute-done.5 = f32[72,128]{1,0:T(8,128)S(1)} collective-permute-done((f32[72,128]{1,0:T(8,128)S(1)}, f32[72,128]{1,0:T(8,128)S(1)}, u32[]{:S(2)}, u32[]{:S(2)}) %collective-permute-start.5) | collective-permute-done | bytes 36896 | tf_op jit(solution)/shard_map/ppermute | solution.py:157
  36.3 0.9 %collective-permute-start.10 = (f32[72,128]{1,0:T(8,128)S(1)}, f32[72,128]{1,0:T(8,128)S(1)}, u32[]{:S(2)}, u32[]{:S(2)}) collective-permute-start(f32[72,128]{1,0:T(8,128)S(1)} %add_add_fusion), channel_id=1, source_target_pairs={{0,24},{8,0},{16,8},{24,16},{1,25},{9,1},{17,9},{25,17},{2,26},{10... | collective-permute-start | bytes 110600 | tf_op jit(solution)/shard_map/ppermute | solution.py:157
  37.2 0.5 %collective-permute-start.9 = (f32[72,128]{1,0:T(8,128)S(1)}, f32[72,128]{1,0:T(8,128)S(1)}, u32[]{:S(2)}, u32[]{:S(2)}) collective-permute-start(f32[72,128]{1,0:T(8,128)S(1)} %add_add_fusion), channel_id=1, source_target_pairs={{0,16},{8,24},{16,0},{24,8},{1,17},{9,25},{17,1},{25,9},{2,18},{10... | collective-permute-start | bytes 110600 | tf_op jit(solution)/shard_map/ppermute | solution.py:157
  37.8 0.2 collective-permute-start.8
  37.9 0.0 copy-done.1
  37.9 0.1 fusion.6
  38.0 1.1 %collective-permute-done.10 = f32[72,128]{1,0:T(8,128)S(1)} collective-permute-done((f32[72,128]{1,0:T(8,128)S(1)}, f32[72,128]{1,0:T(8,128)S(1)}, u32[]{:S(2)}, u32[]{:S(2)}) %collective-permute-start.10) | collective-permute-done | bytes 36896 | tf_op jit(solution)/shard_map/ppermute | solution.py:157
  39.1 2.5 %collective-permute-done.9 = f32[72,128]{1,0:T(8,128)S(1)} collective-permute-done((f32[72,128]{1,0:T(8,128)S(1)}, f32[72,128]{1,0:T(8,128)S(1)}, u32[]{:S(2)}, u32[]{:S(2)}) %collective-permute-start.9) | collective-permute-done | bytes 36896 | tf_op jit(solution)/shard_map/ppermute | solution.py:157
  41.5 0.0 collective-permute-done.8
  41.6 0.1 reshape.104
  41.7 0.1 fusion.8
  41.8 0.1 fusion.9
  41.9 0.1 maximum_bitcast_fusion
  42.1 0.3 copy.6
  42.4 1.2 %reshape.105 = f32[2,16384]{1,0:T(2,128)} reshape(f32[2,1024,16]{2,1,0:T(8,128)S(1)} %copy.6) | data formatting | bytes 262144 | tf_op jit(solution)/shard_map/reshape | solution.py:232
  43.7 0.7 %fusion.2 = bf16[64,1024]{1,0:T(8,128)(2,1)} fusion(f32[32,1024]{1,0:T(8,128)S(1)} %get-tuple-element.19, f32[32,1024]{1,0:T(8,128)S(1)} %get-tuple-element.18, f32[1024]{0:T(1024)S(1)} %maximum_sqrt_fusion, f32[1024]{0:T(1024)S(1)} %bitcast.62), kind=kLoop, calls=%fused_computation.11 | loop fusion | flops 327680 | bytes 401408 | tf_op jit(solution)/shard_map/convert_element_type | solution.py:247
  (18 shorter events, 0.2 us)
Async XLA Ops:
  0.6 12.9 %copy-start.2 = (s32[2048]{0:T(1024)S(1)}, s32[2048]{0:T(1024)}, u32[]{:S(2)}) copy-start(s32[2048]{0:T(1024)} %param.7) | copy-start | bytes 24580
  10.5 11.6 %collective-permute-start = (f32[256,128]{1,0:T(8,128)}, f32[256,128]{1,0:T(8,128)S(1)}, u32[]{:S(2)}, u32[]{:S(2)}) collective-permute-start(f32[256,128]{1,0:T(8,128)} %get-tuple-element.11), channel_id=1, source_target_pairs={{0,1},{1,0},{2,3},{3,2},{4,5},{5,4},{6,7},{7,6},{8,9},{9,8},{10,11... | collective-permute-start | bytes 393224 | tf_op jit(solution)/shard_map/ppermute | solution.py:157
  17.6 4.6 %copy-start = (f32[256,128]{1,0:T(8,128)S(1)}, f32[256,128]{1,0:T(8,128)}, u32[]{:S(2)}) copy-start(f32[256,128]{1,0:T(8,128)} %get-tuple-element.10) | copy-start | bytes 393220
  17.6 3.9 %collective-permute-start.1 = (f32[2,1024]{1,0:T(2,128)}, f32[2,1024]{1,0:T(2,128)S(1)}, u32[]{:S(2)}, u32[]{:S(2)}) collective-permute-start(f32[2,1024]{1,0:T(2,128)} %get-tuple-element.15), channel_id=1, source_target_pairs={{0,1},{1,0},{2,3},{3,2},{4,5},{5,4},{6,7},{7,6},{8,9},{9,8},{10,11... | collective-permute-start | bytes 24584 | tf_op jit(solution)/shard_map/ppermute | solution.py:157
  22.2 3.1 %copy-start.3 = (bf16[32,1024]{1,0:T(8,128)(2,1)S(1)}, bf16[32,1024]{1,0:T(8,128)(2,1)}, u32[]{:S(2)}) copy-start(bf16[32,1024]{1,0:T(8,128)(2,1)} %get-tuple-element.17) | copy-start | bytes 196612
  22.2 3.5 %collective-permute-start.2 = (f32[72,128]{1,0:T(8,128)S(1)}, f32[72,128]{1,0:T(8,128)S(1)}, u32[]{:S(2)}, u32[]{:S(2)}) collective-permute-start(f32[72,128]{1,0:T(8,128)S(1)} %get-tuple-element.24), channel_id=1, source_target_pairs={{0,8},{8,16},{16,24},{24,0},{1,9},{9,17},{17,25},{25,1},{2,10},{10... | collective-permute-start | bytes 110600 | tf_op jit(solution)/shard_map/ppermute | solution.py:157
  22.3 4.0 %collective-permute-start.3 = (f32[72,128]{1,0:T(8,128)S(1)}, f32[72,128]{1,0:T(8,128)S(1)}, u32[]{:S(2)}, u32[]{:S(2)}) collective-permute-start(f32[72,128]{1,0:T(8,128)S(1)} %get-tuple-element.25), channel_id=1, source_target_pairs={{0,16},{8,24},{16,0},{24,8},{1,17},{9,25},{17,1},{25,9},{2,18},{10... | collective-permute-start | bytes 110600 | tf_op jit(solution)/shard_map/ppermute | solution.py:157
  23.9 3.0 %collective-permute-start.4 = (f32[72,128]{1,0:T(8,128)S(1)}, f32[72,128]{1,0:T(8,128)S(1)}, u32[]{:S(2)}, u32[]{:S(2)}) collective-permute-start(f32[72,128]{1,0:T(8,128)S(1)} %get-tuple-element.26), channel_id=1, source_target_pairs={{0,24},{8,0},{16,8},{24,16},{1,25},{9,1},{17,9},{25,17},{2,26},{10... | collective-permute-start | bytes 110600 | tf_op jit(solution)/shard_map/ppermute | solution.py:157
  25.3 6.3 %collective-permute-start.11 = (bf16[32,1024]{1,0:T(8,128)(2,1)S(1)}, bf16[32,1024]{1,0:T(8,128)(2,1)S(1)}, u32[]{:S(2)}, u32[]{:S(2)}) collective-permute-start(bf16[32,1024]{1,0:T(8,128)(2,1)S(1)} %copy-done.3), channel_id=1, source_target_pairs={{0,1},{1,0},{2,3},{3,2},{4,5},{5,4},{6,7},{7,6},{8,9},{9,8},{10,11... | collective-permute-start | bytes 196616 | tf_op jit(solution)/shard_map/ppermute | solution.py:157
  26.9 5.6 %collective-permute-start.7 = (f32[72,128]{1,0:T(8,128)S(1)}, f32[72,128]{1,0:T(8,128)S(1)}, u32[]{:S(2)}, u32[]{:S(2)}) collective-permute-start(f32[72,128]{1,0:T(8,128)S(1)} %fusion.16), channel_id=1, source_target_pairs={{0,6},{2,0},{4,2},{6,4},{1,7},{3,1},{5,3},{7,5},{8,14},{10,8},{12,... | collective-permute-start | bytes 110600 | tf_op jit(solution)/shard_map/ppermute | solution.py:157
  30.6 4.9 %collective-permute-start.6 = (f32[72,128]{1,0:T(8,128)S(1)}, f32[72,128]{1,0:T(8,128)S(1)}, u32[]{:S(2)}, u32[]{:S(2)}) collective-permute-start(f32[72,128]{1,0:T(8,128)S(1)} %fusion.16), channel_id=1, source_target_pairs={{0,4},{2,6},{4,0},{6,2},{1,5},{3,7},{5,1},{7,3},{8,12},{10,14},{12... | collective-permute-start | bytes 110600 | tf_op jit(solution)/shard_map/ppermute | solution.py:157
  30.6 5.8 %collective-permute-start.5 = (f32[72,128]{1,0:T(8,128)S(1)}, f32[72,128]{1,0:T(8,128)S(1)}, u32[]{:S(2)}, u32[]{:S(2)}) collective-permute-start(f32[72,128]{1,0:T(8,128)S(1)} %fusion.16), channel_id=1, source_target_pairs={{0,2},{2,4},{4,6},{6,0},{1,3},{3,5},{5,7},{7,1},{8,10},{10,12},{12... | collective-permute-start | bytes 110600 | tf_op jit(solution)/shard_map/ppermute | solution.py:157
  31.6 6.3 %copy-start.1 = (f32[32,1024]{1,0:T(8,128)S(1)}, f32[32,1024]{1,0:T(8,128)}, u32[]{:S(2)}) copy-start(f32[32,1024]{1,0:T(8,128)} %get-tuple-element.16) | copy-start | bytes 393220
  36.3 2.7 %collective-permute-start.10 = (f32[72,128]{1,0:T(8,128)S(1)}, f32[72,128]{1,0:T(8,128)S(1)}, u32[]{:S(2)}, u32[]{:S(2)}) collective-permute-start(f32[72,128]{1,0:T(8,128)S(1)} %add_add_fusion), channel_id=1, source_target_pairs={{0,24},{8,0},{16,8},{24,16},{1,25},{9,1},{17,9},{25,17},{2,26},{10... | collective-permute-start | bytes 110600 | tf_op jit(solution)/shard_map/ppermute | solution.py:157
  37.2 4.3 %collective-permute-start.9 = (f32[72,128]{1,0:T(8,128)S(1)}, f32[72,128]{1,0:T(8,128)S(1)}, u32[]{:S(2)}, u32[]{:S(2)}) collective-permute-start(f32[72,128]{1,0:T(8,128)S(1)} %add_add_fusion), channel_id=1, source_target_pairs={{0,16},{8,24},{16,0},{24,8},{1,17},{9,25},{17,1},{25,9},{2,18},{10... | collective-permute-start | bytes 110600 | tf_op jit(solution)/shard_map/ppermute | solution.py:157
  37.8 3.8 %collective-permute-start.8 = (f32[72,128]{1,0:T(8,128)S(1)}, f32[72,128]{1,0:T(8,128)S(1)}, u32[]{:S(2)}, u32[]{:S(2)}) collective-permute-start(f32[72,128]{1,0:T(8,128)S(1)} %add_add_fusion), channel_id=1, source_target_pairs={{0,8},{8,16},{16,24},{24,0},{1,9},{9,17},{17,25},{25,1},{2,10},{10... | collective-permute-start | bytes 110600 | tf_op jit(solution)/shard_map/ppermute | solution.py:157

commit v2 on v1

--- a/solution.py
+++ b/solution.py
@@ -11,6 +11,10 @@
 STRIDE = 16
 LANES = 128
 HIGH = GENES // (STRIDE * LANES)
+HALF = LANES // 2
+STRIDE_BITS = STRIDE.bit_length() - 1
+ROW_BITS = (STRIDE * LANES).bit_length() - 1
+HALF_BITS = (STRIDE * HALF).bit_length() - 1
 
 target_sum = 10000.0
 var_floor = 0.01
@@ -24,9 +28,9 @@
     return jnp.broadcast_to(ref[pl.ds(row, 1), pl.ds(start, width)], (16, width)).astype(bf16)
 
 
-def one_hot_lanes(low16, ids, width):
+def one_hot_lanes(low16, ids, lanes):
     groups = []
-    for g in range(LANES // 16):
+    for g in range(lanes // 16):
         hit = low16 == (ids + bf16(16.0 * g))
         groups.append(jnp.where(hit, bf16(1.0), bf16(0.0)))
     return groups
@@ -45,33 +49,37 @@
     columns = columns_ref[...]
     count = jnp.where(live, counts_ref[...], 0).astype(f32)
     count_s[...] = count
-    low_s[...] = ((columns // STRIDE) % LANES).astype(f32)
-    high_s[...] = jnp.where(live, columns // (STRIDE * LANES), -1).astype(f32)
-    off_s[...] = (columns % STRIDE).astype(f32)
+    low_s[...] = ((columns >> STRIDE_BITS) & (HALF - 1)).astype(f32)
+    row = (columns >> ROW_BITS) + ((columns >> HALF_BITS) & 1) * HIGH
+    high_s[...] = jnp.where(live, row, -1).astype(f32)
+    off_s[...] = (columns & (STRIDE - 1)).astype(f32)
     library = jnp.sum(count, axis=1, keepdims=True)
     scale_ref[...] = jnp.broadcast_to(target_sum / library, (rows, LANES))
     width = min(256, slots)
     ids = lax.broadcasted_iota(jnp.int32, (16, width), 0).astype(f32).astype(bf16)
 
     def one_cell(c):
-        acc = jnp.zeros((2 * HIGH, LANES), f32)
+        acc = jnp.zeros((4 * HIGH, HALF), f32)
         for start in range(0, slots, width):
             low16 = tile_of_rows(low_s, c, start, width)
             high16 = tile_of_rows(high_s, c, start, width)
             off16 = tile_of_rows(off_s, c, start, width)
             count16 = tile_of_rows(count_s, c, start, width)
-            table = jnp.concatenate(one_hot_lanes(low16, ids, width), axis=0)
-            hit = high16 == ids
+            table = jnp.concatenate(one_hot_lanes(low16, ids, HALF), axis=0)
+            hits = [high16 == ids, high16 == ids + bf16(float(HIGH))]
             payload = jnp.concatenate(
-                [jnp.where(hit, off16, bf16(0.0)), jnp.where(hit, count16, bf16(0.0))], axis=0
+                [jnp.where(hit, part, bf16(0.0)) for part in (off16, count16) for hit in hits],
+                axis=0,
             )
             acc = acc + lax.dot_general(
                 payload, table, (((1,), (1,)), ((), ())), preferred_element_type=f32
             )
         base = pl.multiple_of(c * 2 * HIGH, 2 * HIGH)
-        compact_ref[pl.ds(base, HIGH), :] = acc[:HIGH]
+        off = jnp.concatenate([acc[:HIGH], acc[HIGH:2 * HIGH]], axis=1)
+        count = jnp.concatenate([acc[2 * HIGH:3 * HIGH], acc[3 * HIGH:]], axis=1)
+        compact_ref[pl.ds(base, HIGH), :] = off
         compact_ref[pl.ds(base + HIGH, HIGH), :] = jnp.log(
-            f32(1.0) + acc[HIGH:] * scale_ref[pl.ds(c, 1), :]
+            f32(1.0) + count * scale_ref[pl.ds(c, 1), :]
         )
 
     def cells(step, carry):
@@ -81,28 +89,31 @@
 
     lax.fori_loop(0, rows // 4, cells, 0)
 
-    def offsets(o, carry):
-        o_f = o.astype(f32)
-        total = jnp.zeros((HIGH, LANES), f32)
-        square = jnp.zeros((HIGH, LANES), f32)
+    own_high = HIGH // owners
+    together = 4
+
+    def offsets(step, carry):
+        first = step * together
+        totals = [jnp.zeros((HIGH, LANES), f32)] * together
+        squares = [jnp.zeros((HIGH, LANES), f32)] * together
         for c in range(rows):
             off = compact_ref[pl.ds(c * 2 * HIGH, HIGH), :]
             value = compact_ref[pl.ds(c * 2 * HIGH + HIGH, HIGH), :]
-            value = jnp.where(off == o_f, value, f32(0.0))
-            total = total + value
-            square = square + value * value
-        total_s[0] = total
-        total_s[1] = square
-        own_high = HIGH // owners
-        for d in range(owners):
-            start = lax.rem(owner_ref[0] + d, owners) * own_high
-            for s in range(2):
-                total_refs[d][pl.ds((o * 2 + s) * own_high, own_high), :] = total_s[
-                    s, pl.ds(start, own_high), :
-                ]
+            for u in range(together):
+                mine = jnp.where(off == (first + u).astype(f32), value, f32(0.0))
+                totals[u] = totals[u] + mine
+                squares[u] = squares[u] + mine * mine
+        for u in range(together):
+            total_s[0] = totals[u]
+            total_s[1] = squares[u]
+            for d in range(owners):
+                start = lax.rem(owner_ref[0] + d, owners) * own_high
+                for s in range(2):
+                    target = ((first + u) * 2 + s) * own_high
+                    total_refs[d][pl.ds(target, own_high), :] = total_s[s, pl.ds(start, own_high), :]
         return carry
 
-    lax.fori_loop(0, STRIDE, offsets, 0)
+    lax.fori_loop(0, STRIDE // together, offsets, 0)
 
 
 def select_kernel(owner_ref, compact_ref, scale_ref, selected_ref, *refs, owners):
@@ -110,7 +121,8 @@
     sum_refs = refs[owners:2 * owners]
     pairs_s = refs[2 * owners]
     rows = scale_ref.shape[0]
-    share = selected_ref.shape[1]
+    share = selected_ref.shape[1] // owners
+    share_rows = share // LANES
     width = min(256, share)
     for h in range(HIGH):
         lanes = pl.ds((h % 2) * LANES, LANES)
@@ -125,14 +137,15 @@
     for d in range(owners):
         owner = lax.rem(owner_ref[0] + d, owners)
         for start in range(0, share, width):
-            picked = selected_ref[pl.ds(owner, 1), pl.ds(start, width)]
+            place = pl.multiple_of(owner * share + start, LANES)
+            picked = selected_ref[:, pl.ds(place, width)]
             low16 = jnp.broadcast_to(
-                ((picked // STRIDE) % LANES).astype(f32), (16, width)
+                ((picked >> STRIDE_BITS) & (LANES - 1)).astype(f32), (16, width)
             ).astype(bf16)
             high16 = jnp.broadcast_to(
-                (picked // (STRIDE * LANES)).astype(f32), (16, width)
+                (picked >> ROW_BITS).astype(f32), (16, width)
             ).astype(bf16)
-            low_hot = one_hot_lanes(low16, ids, width)
+            low_hot = one_hot_lanes(low16, ids, LANES)
             acc = jnp.zeros((3 * rows, width), f32)
             for pair in range(HIGH // 2):
                 parts = []
@@ -142,19 +155,49 @@
                 acc = acc + jnp.dot(
                     pairs_s[pair], jnp.concatenate(parts, axis=0), preferred_element_type=f32
                 )
-            off = (picked % STRIDE).astype(f32)
+            off = (picked & (STRIDE - 1)).astype(f32)
             value = acc[rows:2 * rows] + acc[2 * rows:]
             dense = jnp.where(acc[:rows] == off, value, f32(0.0))
             dense_refs[d][:, pl.ds(start, width)] = dense.astype(dense_refs[d].dtype)
-            sum_refs[d][pl.ds(0, 1), pl.ds(start, width)] = jnp.sum(dense, axis=0, keepdims=True)
-            sum_refs[d][pl.ds(1, 1), pl.ds(start, width)] = jnp.sum(
-                dense * dense, axis=0, keepdims=True
-            )
+            stats = [
+                jnp.sum(dense, axis=0, keepdims=True),
+                jnp.sum(dense * dense, axis=0, keepdims=True),
+            ]
+            for s in range(2):
+                for q in range(width // LANES):
+                    target = s * share_rows + start // LANES + q
+                    sum_refs[d][pl.ds(target, 1), :] = stats[s][:, q * LANES:(q + 1) * LANES]
 
 
 def shift(value, axis, d):
     n = lax.axis_size(axis)
     return lax.ppermute(value, axis, [(s, (s + d) % n) for s in range(n)])
+
+
+def paired(n):
+    return n & (n - 1) == 0
+
+
+def exchange(value, axis, d):
+    n = lax.axis_size(axis)
+    if not paired(n):
+        return shift(value, axis, d)
+    return lax.ppermute(value, axis, [(s, s ^ d) for s in range(n)])
+
+
+def tree_sum(terms):
+    while len(terms) > 1:
+        last = terms[len(terms) - len(terms) % 2:]
+        terms = [terms[i] + terms[i + 1] for i in range(0, len(terms) - 1, 2)] + last
+    return terms[0]
+
+
+def target_of(place, d, n):
+    return place ^ d if paired(n) else lax.rem(place + d, n)
+
+
+def slot_of(place, i, n):
+    return place ^ i if paired(n) else lax.rem(place + n - i, n)
 
 
 def per_device(columns, counts, nnz_count, selected):
@@ -191,12 +234,12 @@
         functools.partial(select_kernel, owners=owners),
         out_shape=[jax.ShapeDtypeStruct((rows, share), f32)]
         + [jax.ShapeDtypeStruct((rows, share), bf16)] * (owners - 1)
-        + [jax.ShapeDtypeStruct((2, share), f32)] * owners,
+        + [jax.ShapeDtypeStruct((2 * share // LANES, LANES), f32)] * owners,
         in_specs=[smem, vmem, vmem, vmem],
         out_specs=[vmem] * (2 * owners),
         scratch_shapes=[pltpu.VMEM((HIGH // 2, 3 * rows, 2 * LANES), bf16)],
         name="select",
-    )(owner_arg, compact, scale, selected.reshape(owners, share))
+    )(owner_arg, compact, scale, selected.reshape(1, sel))
     dense, picked_sums = picked[:owners], picked[owners:]
     moved_picked = [shift(picked_sums[d], "gz", d) for d in range(1, owners)]
     moved_dense = [shift(dense[d], "gz", d) for d in range(1, owners)]
@@ -204,35 +247,28 @@
     gene_sums = functools.reduce(jnp.add, [sums[0]] + moved_sums)
     sel_sums = functools.reduce(jnp.add, [picked_sums[0]] + moved_picked)
     chunk_rows = sum_rows // outer
-    sel_part = sel_sums.reshape(2, outer, share // outer).transpose(1, 0, 2).reshape(outer, -1)
-    extra = -(-sel_part.shape[1] // (8 * LANES)) * 8
-    sel_part = jnp.pad(sel_part, ((0, 0), (0, extra * LANES - sel_part.shape[1])))
-    both = jnp.concatenate(
-        [gene_sums.reshape(outer, chunk_rows, LANES), sel_part.reshape(outer, extra, LANES)], axis=1
-    )
-
-    def chunk(index):
-        return lax.dynamic_index_in_dim(both, index, 0, keepdims=False)
+    chunks = gene_sums.reshape(outer, chunk_rows, LANES)
+
+    def chunk(d):
+        return lax.dynamic_index_in_dim(chunks, target_of(place, d, outer), 0, keepdims=False)
 
     part = functools.reduce(
-        jnp.add,
-        [chunk(place)] + [shift(chunk(lax.rem(place + d, outer)), "gx", d) for d in range(1, outer)],
-    )
-    part = functools.reduce(jnp.add, [part] + [shift(part, "gy", d) for d in range(1, middle)])
-    held = jnp.stack([part] + [shift(part, "gx", d) for d in range(1, outer)])
+        jnp.add, [chunk(0)] + [exchange(chunk(d), "gx", d) for d in range(1, outer)]
+    )
+    part = jnp.concatenate([part, sel_sums], axis=0)
+    part = tree_sum([part] + [exchange(part, "gy", d) for d in range(1, middle)])
+    held = jnp.stack([part] + [exchange(part, "gx", d) for d in range(1, outer)])
     full = jnp.stack(
         [
-            lax.dynamic_index_in_dim(held, lax.rem(place + outer - i, outer), 0, keepdims=False)
+            lax.dynamic_index_in_dim(held[:, :chunk_rows], slot_of(place, i, outer), 0, keepdims=False)
             for i in range(outer)
         ]
     )
-    genes = full[:, :chunk_rows].reshape(STRIDE, 2, own_high * LANES)
+    genes = full.reshape(STRIDE, 2, own_high * LANES)
     mean = genes[:, 0] / cells
     variance = genes[:, 1] / cells - mean * mean
     gene_stats = jnp.stack([mean, variance]).transpose(0, 2, 1).reshape(2, -1)
-    part_size = share // outer
-    sel_full = full[:, chunk_rows:].reshape(outer, -1)[:, :2 * part_size]
-    sel_full = sel_full.reshape(outer, 2, part_size).transpose(1, 0, 2).reshape(2, share)
+    sel_full = jnp.sum(held[:, chunk_rows:], axis=0).reshape(2, share)
     sel_mean = sel_full[0] / cells
     sel_variance = sel_full[1] / cells - sel_mean * sel_mean
     sel_scale = jnp.sqrt(jnp.maximum(sel_variance, var_floor))

time: 44.6 us -> 40.7 us (0.913)
  Pallas kernels: 13.3 us -> 10.2 us
  waiting for transfers between devices: 13.3 us -> 12.2 us
  starting transfers between devices: 12.7 us -> 13.6 us
  local copies, waits for them, and re-layouts: 2.36 us -> 1.7 us
    ppermute x0 -> x9, starting transfers between devices: none -> 8.57 us  [exchange(): return lax.ppermute(value, axis, [(s, s ^ d) for s in range(n)])]
    ppermute x12 -> x3, waiting for transfers between devices: 13.3 us -> 5.54 us  [shift(): return lax.ppermute(value, axis, [(s, (s + d) % n) for s in range(n)])]
    ppermute x12 -> x3, starting transfers between devices: 12.7 us -> 5.03 us  [shift(): return lax.ppermute(value, axis, [(s, (s + d) % n) for s in range(n)])]
    ppermute x0 -> x9, waiting for transfers between devices: none -> 6.67 us  [exchange(): return lax.ppermute(value, axis, [(s, s ^ d) for s in range(n)])]
    pallas_call x1, Pallas kernels: 9.88 us -> 6.77 us  [per_device(): pl.pallas_call(functools.partial(scatter_kernel, owners=owners), out_shap...]
    add x1, other arithmetic: 0.02 us -> 0.92 us  [per_device(): gene_sums = functools.reduce(jnp.add, [sums[0]] + moved_sums)]
    add x1, other arithmetic: 0.7 us -> 0.01 us  [per_device(): sel_sums = functools.reduce(jnp.add, [picked_sums[0]] + moved_picked)]
    reshape x4 -> x1, local copies, waits for them, and re-layouts: 0.71 us -> 0.07 us  [per_device(): genes = full.reshape(STRIDE, 2, own_high * LANES)]
  transfers between devices with their start and end apart: 12 -> 12, of which waited for: 8 -> 6; matrix products, arithmetic and copies ran while one was open for 3% -> 0% of each run, Pallas kernels for 8% -> 8%
where the time goes in v2:
time: 40.7 us; the launch traced here: 40.5 us
  starting transfers between devices  13.6 us (33%)
  waiting for transfers between devices  12.2 us (30%)
  Pallas kernels  10.2 us (25%)
  other arithmetic  2.04 us (5%)
  local copies, waits for them, and re-layouts  1.7 us (4%)
  between operations  0.81 us (2%)
    ppermute x9, starting transfers between devices, exchange(): return lax.ppermute(value, axis, [(s, s ^ d) for s in range(n)])  8.57 us
    pallas_call x1, Pallas kernels, per_device(): pl.pallas_call(functools.partial(scatter_kernel, owners=owners), out_shap...  6.77 us
    ppermute x9, waiting for transfers between devices, exchange(): return lax.ppermute(value, axis, [(s, s ^ d) for s in range(n)])  6.67 us
    ppermute x3, waiting for transfers between devices, shift(): return lax.ppermute(value, axis, [(s, (s + d) % n) for s in range(n)])  5.54 us
    ppermute x3, starting transfers between devices, shift(): return lax.ppermute(value, axis, [(s, (s + d) % n) for s in range(n)])  5.03 us
    pallas_call x1, Pallas kernels, per_device(): pl.pallas_call(functools.partial(select_kernel, owners=owners), out_shape...  3.41 us
    reshape x1, local copies, waits for them, and re-layouts, per_device(): gene_stats = jnp.stack([mean, variance]).transpose(0, 2, 1).reshape(2, -1)  1.23 us
    add x1, other arithmetic, per_device(): gene_sums = functools.reduce(jnp.add, [sums[0]] + moved_sums)  0.92 us
  transfers between devices with their start and end apart: 12, of which 6 were waited for; matrix products, arithmetic and copies ran while one was open for 0% of the time, Pallas kernels for 8%

profile of v2, /device:TPU:0, one launch (start us, length us, event | category | flops | bytes accessed | tf_op | source)
XLA Modules:
  0.0 40.5 jit_solution(3766332200749875836)
XLA Ops:
  0.6 6.8 %scatter.1 = (f32[1024,128]{1,0:T(8,128)}, f32[32,128]{1,0:T(8,128)}, f32[256,128]{1,0:T(8,128)}, f32[256,128]{1,0:T(8,128)}) custom-call(s32[1]{0:T(128)} %bitcast.owner_ref, s32[32,2048]{1,0:T(8,128)} %columns_ref.1, s32[32,2048]{1,0:T(8,128)} %counts_ref.1, s32[1,32]{1,0:T(1,128)} %bitcast.62), custom_call_target="tpu_custom_call" | custom-call | tf_op jit(solution)/shard_map/scatter/pallas_call | solution.py:219
  7.4 3.0 %collective-permute-start = (f32[256,128]{1,0:T(8,128)}, f32[256,128]{1,0:T(8,128)S(1)}, u32[]{:S(2)}, u32[]{:S(2)}) collective-permute-start(f32[256,128]{1,0:T(8,128)} %get-tuple-element.11), channel_id=1, source_target_pairs={{0,1},{1,0},{2,3},{3,2},{4,5},{5,4},{6,7},{7,6},{8,9},{9,8},{10,11... | collective-permute-start | bytes 393224 | tf_op jit(solution)/shard_map/ppermute | solution.py:174
  10.4 3.7 %collective-permute-done = f32[256,128]{1,0:T(8,128)S(1)} collective-permute-done((f32[256,128]{1,0:T(8,128)}, f32[256,128]{1,0:T(8,128)S(1)}, u32[]{:S(2)}, u32[]{:S(2)}) %collective-permute-start) | collective-permute-done | bytes 131104 | tf_op jit(solution)/shard_map/ppermute | solution.py:174
  14.1 0.9 %add.55 = f32[256,128]{1,0:T(8,128)S(1)} add(f32[256,128]{1,0:T(8,128)} %get-tuple-element.10, f32[256,128]{1,0:T(8,128)S(1)} %collective-permute-done) | non-fusion elementwise | flops 32768 | bytes 393216 | tf_op jit(solution)/shard_map/add | solution.py:247
  15.1 0.1 collective-permute-start.1
  15.1 1.8 %collective-permute-start.3 = (f32[64,128]{1,0:T(8,128)S(1)}, f32[64,128]{1,0:T(8,128)S(1)}, u32[]{:S(2)}, u32[]{:S(2)}) collective-permute-start(f32[64,128]{1,0:T(8,128)S(1)} %get-tuple-element.25), channel_id=1, source_target_pairs={{0,24},{8,16},{16,8},{24,0},{1,25},{9,17},{17,9},{25,1},{2,26},{10... | collective-permute-start | bytes 98312 | tf_op jit(solution)/shard_map/ppermute | solution.py:185
  17.0 0.3 collective-permute-start.2
  17.3 3.4 %select.5 = (f32[32,1024]{1,0:T(8,128)}, bf16[32,1024]{1,0:T(8,128)(2,1)}, f32[16,128]{1,0:T(8,128)}, f32[16,128]{1,0:T(8,128)}) custom-call(s32[1]{0:T(128)} %bitcast.owner_ref, f32[1024,128]{1,0:T(8,128)} %get-tuple-element.12.compact_ref, f32[32,128]{1,0:T(8,128)} %get-tuple-element.13.scale_ref, s32[1,2048]{1,0:T(1,128)} %bitcast.61), custom_call_target="tpu_custom_call" | custom-call | tf_op jit(solution)/shard_map/select/pallas_call | solution.py:233
  20.7 1.7 %collective-permute-start.4 = (f32[16,128]{1,0:T(8,128)}, f32[16,128]{1,0:T(8,128)S(1)}, u32[]{:S(2)}, u32[]{:S(2)}) collective-permute-start(f32[16,128]{1,0:T(8,128)} %get-tuple-element.15), channel_id=1, source_target_pairs={{0,1},{1,0},{2,3},{3,2},{4,5},{5,4},{6,7},{7,6},{8,9},{9,8},{10,11... | collective-permute-start | bytes 24584 | tf_op jit(solution)/shard_map/ppermute | solution.py:174
  22.4 0.3 collective-permute-start.11
  22.7 0.0 copy-start.1
  22.7 1.8 %collective-permute-done.4 = f32[16,128]{1,0:T(8,128)S(1)} collective-permute-done((f32[16,128]{1,0:T(8,128)}, f32[16,128]{1,0:T(8,128)S(1)}, u32[]{:S(2)}, u32[]{:S(2)}) %collective-permute-start.4) | collective-permute-done | bytes 8224 | tf_op jit(solution)/shard_map/ppermute | solution.py:174
  24.5 0.0 copy-done.1
  24.5 0.0 collective-permute-done.1
  24.6 0.0 collective-permute-done.3
  24.6 0.0 collective-permute-done.2
  24.6 2.9 %collective-permute-start.6 = (f32[80,128]{1,0:T(8,128)S(1)}, f32[80,128]{1,0:T(8,128)S(1)}, u32[]{:S(2)}, u32[]{:S(2)}) collective-permute-start(f32[80,128]{1,0:T(8,128)S(1)} %pad_maximum_fusion.2), channel_id=1, source_target_pairs={{0,4},{2,6},{4,0},{6,2},{1,5},{3,7},{5,1},{7,3},{8,12},{10,14},{12... | collective-permute-start | bytes 122888 | tf_op jit(solution)/shard_map/ppermute | solution.py:185
  27.5 1.4 %collective-permute-start.7 = (f32[80,128]{1,0:T(8,128)S(1)}, f32[80,128]{1,0:T(8,128)S(1)}, u32[]{:S(2)}, u32[]{:S(2)}) collective-permute-start(f32[80,128]{1,0:T(8,128)S(1)} %pad_maximum_fusion.2), channel_id=1, source_target_pairs={{0,6},{2,4},{4,2},{6,0},{1,7},{3,5},{5,3},{7,1},{8,14},{10,12},{12... | collective-permute-start | bytes 122888 | tf_op jit(solution)/shard_map/ppermute | solution.py:185
  28.8 0.2 collective-permute-start.5
  29.1 0.0 collective-permute-done.11
  29.1 0.0 copy-start
  29.1 0.6 %collective-permute-done.6 = f32[80,128]{1,0:T(8,128)S(1)} collective-permute-done((f32[80,128]{1,0:T(8,128)S(1)}, f32[80,128]{1,0:T(8,128)S(1)}, u32[]{:S(2)}, u32[]{:S(2)}) %collective-permute-start.6) | collective-permute-done | bytes 40992 | tf_op jit(solution)/shard_map/ppermute | solution.py:185
  29.7 3.6 %collective-permute-done.7 = f32[80,128]{1,0:T(8,128)S(1)} collective-permute-done((f32[80,128]{1,0:T(8,128)S(1)}, f32[80,128]{1,0:T(8,128)S(1)}, u32[]{:S(2)}, u32[]{:S(2)}) %collective-permute-start.7) | collective-permute-done | bytes 40992 | tf_op jit(solution)/shard_map/ppermute | solution.py:185
  33.3 0.0 collective-permute-done.5
  33.3 0.1 collective-permute-start.10
  33.4 1.6 %collective-permute-start.9 = (f32[80,128]{1,0:T(8,128)S(1)}, f32[80,128]{1,0:T(8,128)S(1)}, u32[]{:S(2)}, u32[]{:S(2)}) collective-permute-start(f32[80,128]{1,0:T(8,128)S(1)} %add_add_fusion), channel_id=1, source_target_pairs={{0,16},{8,24},{16,0},{24,8},{1,17},{9,25},{17,1},{25,9},{2,18},{10... | collective-permute-start | bytes 122888 | tf_op jit(solution)/shard_map/ppermute | solution.py:185
  35.0 0.3 collective-permute-start.8
  35.2 0.0 copy-done
  35.2 0.1 fusion.6
  35.3 1.9 %collective-permute-done.10 = f32[80,128]{1,0:T(8,128)S(1)} collective-permute-done((f32[80,128]{1,0:T(8,128)S(1)}, f32[80,128]{1,0:T(8,128)S(1)}, u32[]{:S(2)}, u32[]{:S(2)}) %collective-permute-start.10) | collective-permute-done | bytes 40992 | tf_op jit(solution)/shard_map/ppermute | solution.py:185
  37.2 0.6 %collective-permute-done.9 = f32[80,128]{1,0:T(8,128)S(1)} collective-permute-done((f32[80,128]{1,0:T(8,128)S(1)}, f32[80,128]{1,0:T(8,128)S(1)}, u32[]{:S(2)}, u32[]{:S(2)}) %collective-permute-start.9) | collective-permute-done | bytes 40992 | tf_op jit(solution)/shard_map/ppermute | solution.py:185
  37.8 0.0 collective-permute-done.8
  37.9 0.1 reshape.86
  38.0 0.1 fusion.8
  38.1 0.1 fusion.9
  38.1 0.1 maximum_bitcast_fusion
  38.3 0.3 copy.6
  38.6 1.2 %reshape.87 = f32[2,16384]{1,0:T(2,128)} reshape(f32[2,1024,16]{2,1,0:T(8,128)S(1)} %copy.6) | data formatting | bytes 262144 | tf_op jit(solution)/shard_map/reshape | solution.py:270
  39.8 0.7 %fusion.2 = bf16[64,1024]{1,0:T(8,128)(2,1)} fusion(f32[32,1024]{1,0:T(8,128)S(1)} %get-tuple-element.19, f32[32,1024]{1,0:T(8,128)S(1)} %get-tuple-element.18, f32[1024]{0:T(1024)S(1)} %fusion.15, f32[1024]{0:T(1024)S(1)} %fusion.16), kind=kLoop, calls=%fused_computation.7 | loop fusion | flops 327680 | bytes 401408 | tf_op jit(solution)/shard_map/convert_element_type | solution.py:283
  (13 shorter events, 0.1 us)
Async XLA Ops:
  7.4 6.7 %collective-permute-start = (f32[256,128]{1,0:T(8,128)}, f32[256,128]{1,0:T(8,128)S(1)}, u32[]{:S(2)}, u32[]{:S(2)}) collective-permute-start(f32[256,128]{1,0:T(8,128)} %get-tuple-element.11), channel_id=1, source_target_pairs={{0,1},{1,0},{2,3},{3,2},{4,5},{5,4},{6,7},{7,6},{8,9},{9,8},{10,11... | collective-permute-start | bytes 393224 | tf_op jit(solution)/shard_map/ppermute | solution.py:174
  15.1 9.5 %collective-permute-start.1 = (f32[64,128]{1,0:T(8,128)S(1)}, f32[64,128]{1,0:T(8,128)S(1)}, u32[]{:S(2)}, u32[]{:S(2)}) collective-permute-start(f32[64,128]{1,0:T(8,128)S(1)} %get-tuple-element.24), channel_id=1, source_target_pairs={{0,8},{8,0},{16,24},{24,16},{1,9},{9,1},{17,25},{25,17},{2,10},{10... | collective-permute-start | bytes 98312 | tf_op jit(solution)/shard_map/ppermute | solution.py:185
  15.1 9.4 %collective-permute-start.3 = (f32[64,128]{1,0:T(8,128)S(1)}, f32[64,128]{1,0:T(8,128)S(1)}, u32[]{:S(2)}, u32[]{:S(2)}) collective-permute-start(f32[64,128]{1,0:T(8,128)S(1)} %get-tuple-element.25), channel_id=1, source_target_pairs={{0,24},{8,16},{16,8},{24,0},{1,25},{9,17},{17,9},{25,1},{2,26},{10... | collective-permute-start | bytes 98312 | tf_op jit(solution)/shard_map/ppermute | solution.py:185
  17.0 7.6 %collective-permute-start.2 = (f32[64,128]{1,0:T(8,128)S(1)}, f32[64,128]{1,0:T(8,128)S(1)}, u32[]{:S(2)}, u32[]{:S(2)}) collective-permute-start(f32[64,128]{1,0:T(8,128)S(1)} %get-tuple-element.26), channel_id=1, source_target_pairs={{0,16},{8,24},{16,0},{24,8},{1,17},{9,25},{17,1},{25,9},{2,18},{10... | collective-permute-start | bytes 98312 | tf_op jit(solution)/shard_map/ppermute | solution.py:185
  20.7 3.9 %collective-permute-start.4 = (f32[16,128]{1,0:T(8,128)}, f32[16,128]{1,0:T(8,128)S(1)}, u32[]{:S(2)}, u32[]{:S(2)}) collective-permute-start(f32[16,128]{1,0:T(8,128)} %get-tuple-element.15), channel_id=1, source_target_pairs={{0,1},{1,0},{2,3},{3,2},{4,5},{5,4},{6,7},{7,6},{8,9},{9,8},{10,11... | collective-permute-start | bytes 24584 | tf_op jit(solution)/shard_map/ppermute | solution.py:174
  22.4 6.7 %collective-permute-start.11 = (bf16[32,1024]{1,0:T(8,128)(2,1)}, bf16[32,1024]{1,0:T(8,128)(2,1)S(1)}, u32[]{:S(2)}, u32[]{:S(2)}) collective-permute-start(bf16[32,1024]{1,0:T(8,128)(2,1)} %get-tuple-element.17), channel_id=1, source_target_pairs={{0,1},{1,0},{2,3},{3,2},{4,5},{5,4},{6,7},{7,6},{8,9},{9,8},{10,11... | collective-permute-start | bytes 196616 | tf_op jit(solution)/shard_map/ppermute | solution.py:174
  22.7 1.8 %copy-start.1 = (f32[16,128]{1,0:T(8,128)S(1)}, f32[16,128]{1,0:T(8,128)}, u32[]{:S(2)}) copy-start(f32[16,128]{1,0:T(8,128)} %get-tuple-element.14) | copy-start | bytes 24580
  24.6 5.1 %collective-permute-start.6 = (f32[80,128]{1,0:T(8,128)S(1)}, f32[80,128]{1,0:T(8,128)S(1)}, u32[]{:S(2)}, u32[]{:S(2)}) collective-permute-start(f32[80,128]{1,0:T(8,128)S(1)} %pad_maximum_fusion.2), channel_id=1, source_target_pairs={{0,4},{2,6},{4,0},{6,2},{1,5},{3,7},{5,1},{7,3},{8,12},{10,14},{12... | collective-permute-start | bytes 122888 | tf_op jit(solution)/shard_map/ppermute | solution.py:185
  27.5 5.8 %collective-permute-start.7 = (f32[80,128]{1,0:T(8,128)S(1)}, f32[80,128]{1,0:T(8,128)S(1)}, u32[]{:S(2)}, u32[]{:S(2)}) collective-permute-start(f32[80,128]{1,0:T(8,128)S(1)} %pad_maximum_fusion.2), channel_id=1, source_target_pairs={{0,6},{2,4},{4,2},{6,0},{1,7},{3,5},{5,3},{7,1},{8,14},{10,12},{12... | collective-permute-start | bytes 122888 | tf_op jit(solution)/shard_map/ppermute | solution.py:185
  28.8 4.4 %collective-permute-start.5 = (f32[80,128]{1,0:T(8,128)S(1)}, f32[80,128]{1,0:T(8,128)S(1)}, u32[]{:S(2)}, u32[]{:S(2)}) collective-permute-start(f32[80,128]{1,0:T(8,128)S(1)} %pad_maximum_fusion.2), channel_id=1, source_target_pairs={{0,2},{2,0},{4,6},{6,4},{1,3},{3,1},{5,7},{7,5},{8,10},{10,8},{12,... | collective-permute-start | bytes 122888 | tf_op jit(solution)/shard_map/ppermute | solution.py:185
  29.1 6.2 %copy-start = (f32[32,1024]{1,0:T(8,128)S(1)}, f32[32,1024]{1,0:T(8,128)}, u32[]{:S(2)}) copy-start(f32[32,1024]{1,0:T(8,128)} %get-tuple-element.16) | copy-start | bytes 393220
  33.3 3.9 %collective-permute-start.10 = (f32[80,128]{1,0:T(8,128)S(1)}, f32[80,128]{1,0:T(8,128)S(1)}, u32[]{:S(2)}, u32[]{:S(2)}) collective-permute-start(f32[80,128]{1,0:T(8,128)S(1)} %add_add_fusion), channel_id=1, source_target_pairs={{0,24},{8,16},{16,8},{24,0},{1,25},{9,17},{17,9},{25,1},{2,26},{10... | collective-permute-start | bytes 122888 | tf_op jit(solution)/shard_map/ppermute | solution.py:185
  33.4 4.4 %collective-permute-start.9 = (f32[80,128]{1,0:T(8,128)S(1)}, f32[80,128]{1,0:T(8,128)S(1)}, u32[]{:S(2)}, u32[]{:S(2)}) collective-permute-start(f32[80,128]{1,0:T(8,128)S(1)} %add_add_fusion), channel_id=1, source_target_pairs={{0,16},{8,24},{16,0},{24,8},{1,17},{9,25},{17,1},{25,9},{2,18},{10... | collective-permute-start | bytes 122888 | tf_op jit(solution)/shard_map/ppermute | solution.py:185
  35.0 2.8 %collective-permute-start.8 = (f32[80,128]{1,0:T(8,128)S(1)}, f32[80,128]{1,0:T(8,128)S(1)}, u32[]{:S(2)}, u32[]{:S(2)}) collective-permute-start(f32[80,128]{1,0:T(8,128)S(1)} %add_add_fusion), channel_id=1, source_target_pairs={{0,8},{8,0},{16,24},{24,16},{1,9},{9,1},{17,25},{25,17},{2,10},{10... | collective-permute-start | bytes 122888 | tf_op jit(solution)/shard_map/ppermute | solution.py:185

commit v3 on v2

--- a/solution.py
+++ b/solution.py
@@ -240,11 +240,12 @@
         scratch_shapes=[pltpu.VMEM((HIGH // 2, 3 * rows, 2 * LANES), bf16)],
         name="select",
     )(owner_arg, compact, scale, selected.reshape(1, sel))
+    own_sums, *picked = lax.optimization_barrier((sums[0], *picked))
     dense, picked_sums = picked[:owners], picked[owners:]
     moved_picked = [shift(picked_sums[d], "gz", d) for d in range(1, owners)]
     moved_dense = [shift(dense[d], "gz", d) for d in range(1, owners)]
 
-    gene_sums = functools.reduce(jnp.add, [sums[0]] + moved_sums)
+    gene_sums = functools.reduce(jnp.add, [own_sums] + moved_sums)
     sel_sums = functools.reduce(jnp.add, [picked_sums[0]] + moved_picked)
     chunk_rows = sum_rows // outer
     chunks = gene_sums.reshape(outer, chunk_rows, LANES)

time: 40.7 us -> 36.2 us (0.89)
  waiting for transfers between devices: 12.2 us -> 8.57 us
  other arithmetic: 2.04 us -> 1.14 us
    ppermute x3, waiting for transfers between devices: 5.54 us -> 1.88 us  [shift(): return lax.ppermute(value, axis, [(s, (s + d) % n) for s in range(n)])]
    add x1, other arithmetic: 0.92 us -> 0.02 us  [per_device(): gene_sums = functools.reduce(jnp.add, [own_sums] + moved_sums)]
  transfers between devices with their start and end apart: 12 -> 12, of which waited for: 6 -> 6; matrix products, arithmetic and copies ran while one was open for 0% -> 0% of each run, Pallas kernels for 8% -> 10%
where the time goes in v3:
time: 36.2 us; the launch traced here: 36.1 us
  starting transfers between devices  13.6 us (38%)
  Pallas kernels  10.2 us (28%)
  waiting for transfers between devices  8.57 us (24%)
  local copies, waits for them, and re-layouts  1.71 us (5%)
  other arithmetic  1.14 us (3%)
  between operations  0.83 us (2%)
    ppermute x9, starting transfers between devices, exchange(): return lax.ppermute(value, axis, [(s, s ^ d) for s in range(n)])  8.58 us
    pallas_call x1, Pallas kernels, per_device(): pl.pallas_call(functools.partial(scatter_kernel, owners=owners), out_shap...  6.77 us
    ppermute x9, waiting for transfers between devices, exchange(): return lax.ppermute(value, axis, [(s, s ^ d) for s in range(n)])  6.7 us
    ppermute x3, starting transfers between devices, shift(): return lax.ppermute(value, axis, [(s, (s + d) % n) for s in range(n)])  5.03 us
    pallas_call x1, Pallas kernels, per_device(): pl.pallas_call(functools.partial(select_kernel, owners=owners), out_shape...  3.45 us
    ppermute x3, waiting for transfers between devices, shift(): return lax.ppermute(value, axis, [(s, (s + d) % n) for s in range(n)])  1.88 us
    reshape x1, local copies, waits for them, and re-layouts, per_device(): gene_stats = jnp.stack([mean, variance]).transpose(0, 2, 1).reshape(2, -1)  1.23 us
  transfers between devices with their start and end apart: 12, of which 6 were waited for; matrix products, arithmetic and copies ran while one was open for 0% of the time, Pallas kernels for 10%

profile of v3, /device:TPU:0, one launch (start us, length us, event | category | flops | bytes accessed | tf_op | source)
XLA Modules:
  0.0 36.1 jit_solution(8213717070132878718)
XLA Ops:
  0.6 6.8 %scatter.1 = (f32[1024,128]{1,0:T(8,128)}, f32[32,128]{1,0:T(8,128)}, f32[256,128]{1,0:T(8,128)}, f32[256,128]{1,0:T(8,128)}) custom-call(s32[1]{0:T(128)} %bitcast.owner_ref, s32[32,2048]{1,0:T(8,128)} %columns_ref.1, s32[32,2048]{1,0:T(8,128)} %counts_ref.1, s32[1,32]{1,0:T(1,128)} %bitcast.62), custom_call_target="tpu_custom_call" | custom-call | tf_op jit(solution)/shard_map/scatter/pallas_call | solution.py:219
  7.4 3.0 %collective-permute-start = (f32[256,128]{1,0:T(8,128)}, f32[256,128]{1,0:T(8,128)S(1)}, u32[]{:S(2)}, u32[]{:S(2)}) collective-permute-start(f32[256,128]{1,0:T(8,128)} %get-tuple-element.23), channel_id=1, source_target_pairs={{0,1},{1,0},{2,3},{3,2},{4,5},{5,4},{6,7},{7,6},{8,9},{9,8},{10,11... | collective-permute-start | bytes 393224 | tf_op jit(solution)/shard_map/ppermute | solution.py:174
  10.4 0.0 copy-start
  10.4 3.4 %select.5 = (f32[32,1024]{1,0:T(8,128)}, bf16[32,1024]{1,0:T(8,128)(2,1)}, f32[16,128]{1,0:T(8,128)}, f32[16,128]{1,0:T(8,128)}) custom-call(s32[1]{0:T(128)} %bitcast.owner_ref, f32[1024,128]{1,0:T(8,128)} %get-tuple-element.16.compact_ref, f32[32,128]{1,0:T(8,128)} %get-tuple-element.17.scale_ref, s32[1,2048]{1,0:T(1,128)} %bitcast.61), custom_call_target="tpu_custom_call" | custom-call | tf_op jit(solution)/shard_map/select/pallas_call | solution.py:233
  13.9 0.3 collective-permute-done
  14.1 0.0 copy-done
  14.1 0.0 copy-start.4
  14.1 0.0 copy-start.3
  14.2 0.1 collective-permute-start.1
  14.3 1.8 %collective-permute-start.3 = (f32[64,128]{1,0:T(8,128)S(1)}, f32[64,128]{1,0:T(8,128)S(1)}, u32[]{:S(2)}, u32[]{:S(2)}) collective-permute-start(f32[64,128]{1,0:T(8,128)S(1)} %get-tuple-element.35), channel_id=1, source_target_pairs={{0,24},{8,16},{16,8},{24,0},{1,25},{9,17},{17,9},{25,1},{2,26},{10... | collective-permute-start | bytes 98312 | tf_op jit(solution)/shard_map/ppermute | solution.py:185
  16.1 0.3 collective-permute-start.2
  16.4 0.0 copy-done.4
  16.4 1.7 %collective-permute-start.4 = (f32[16,128]{1,0:T(8,128)S(1)}, f32[16,128]{1,0:T(8,128)S(1)}, u32[]{:S(2)}, u32[]{:S(2)}) collective-permute-start(f32[16,128]{1,0:T(8,128)S(1)} %copy-done.4), channel_id=1, source_target_pairs={{0,1},{1,0},{2,3},{3,2},{4,5},{5,4},{6,7},{7,6},{8,9},{9,8},{10,11... | collective-permute-start | bytes 24584 | tf_op jit(solution)/shard_map/ppermute | solution.py:174
  18.1 0.0 copy-done.3
  18.1 0.3 collective-permute-start.11
  18.4 0.0 copy-start.2
  18.4 1.6 %collective-permute-done.4 = f32[16,128]{1,0:T(8,128)S(1)} collective-permute-done((f32[16,128]{1,0:T(8,128)S(1)}, f32[16,128]{1,0:T(8,128)S(1)}, u32[]{:S(2)}, u32[]{:S(2)}) %collective-permute-start.4) | collective-permute-done | bytes 8224 | tf_op jit(solution)/shard_map/ppermute | solution.py:174
  20.0 0.0 copy-done.2
  20.1 0.0 collective-permute-done.1
  20.1 0.0 collective-permute-done.3
  20.1 0.0 collective-permute-done.2
  20.1 2.9 %collective-permute-start.6 = (f32[80,128]{1,0:T(8,128)S(1)}, f32[80,128]{1,0:T(8,128)S(1)}, u32[]{:S(2)}, u32[]{:S(2)}) collective-permute-start(f32[80,128]{1,0:T(8,128)S(1)} %pad_maximum_fusion.2), channel_id=1, source_target_pairs={{0,4},{2,6},{4,0},{6,2},{1,5},{3,7},{5,1},{7,3},{8,12},{10,14},{12... | collective-permute-start | bytes 122888 | tf_op jit(solution)/shard_map/ppermute | solution.py:185
  23.0 1.3 %collective-permute-start.7 = (f32[80,128]{1,0:T(8,128)S(1)}, f32[80,128]{1,0:T(8,128)S(1)}, u32[]{:S(2)}, u32[]{:S(2)}) collective-permute-start(f32[80,128]{1,0:T(8,128)S(1)} %pad_maximum_fusion.2), channel_id=1, source_target_pairs={{0,6},{2,4},{4,2},{6,0},{1,7},{3,5},{5,3},{7,1},{8,14},{10,12},{12... | collective-permute-start | bytes 122888 | tf_op jit(solution)/shard_map/ppermute | solution.py:185
  24.3 0.2 collective-permute-start.5
  24.6 0.0 collective-permute-done.11
  24.6 0.0 copy-start.1
  24.6 0.6 %collective-permute-done.6 = f32[80,128]{1,0:T(8,128)S(1)} collective-permute-done((f32[80,128]{1,0:T(8,128)S(1)}, f32[80,128]{1,0:T(8,128)S(1)}, u32[]{:S(2)}, u32[]{:S(2)}) %collective-permute-start.6) | collective-permute-done | bytes 40992 | tf_op jit(solution)/shard_map/ppermute | solution.py:185
  25.2 3.6 %collective-permute-done.7 = f32[80,128]{1,0:T(8,128)S(1)} collective-permute-done((f32[80,128]{1,0:T(8,128)S(1)}, f32[80,128]{1,0:T(8,128)S(1)}, u32[]{:S(2)}, u32[]{:S(2)}) %collective-permute-start.7) | collective-permute-done | bytes 40992 | tf_op jit(solution)/shard_map/ppermute | solution.py:185
  28.8 0.0 collective-permute-done.5
  28.8 0.1 collective-permute-start.10
  28.9 1.6 %collective-permute-start.9 = (f32[80,128]{1,0:T(8,128)S(1)}, f32[80,128]{1,0:T(8,128)S(1)}, u32[]{:S(2)}, u32[]{:S(2)}) collective-permute-start(f32[80,128]{1,0:T(8,128)S(1)} %add_add_fusion), channel_id=1, source_target_pairs={{0,16},{8,24},{16,0},{24,8},{1,17},{9,25},{17,1},{25,9},{2,18},{10... | collective-permute-start | bytes 122888 | tf_op jit(solution)/shard_map/ppermute | solution.py:185
  30.5 0.3 collective-permute-start.8
  30.8 0.0 copy-done.1
  30.8 0.1 fusion.6
  30.8 1.9 %collective-permute-done.10 = f32[80,128]{1,0:T(8,128)S(1)} collective-permute-done((f32[80,128]{1,0:T(8,128)S(1)}, f32[80,128]{1,0:T(8,128)S(1)}, u32[]{:S(2)}, u32[]{:S(2)}) %collective-permute-start.10) | collective-permute-done | bytes 40992 | tf_op jit(solution)/shard_map/ppermute | solution.py:185
  32.7 0.6 %collective-permute-done.9 = f32[80,128]{1,0:T(8,128)S(1)} collective-permute-done((f32[80,128]{1,0:T(8,128)S(1)}, f32[80,128]{1,0:T(8,128)S(1)}, u32[]{:S(2)}, u32[]{:S(2)}) %collective-permute-start.9) | collective-permute-done | bytes 40992 | tf_op jit(solution)/shard_map/ppermute | solution.py:185
  33.3 0.0 collective-permute-done.8
  33.4 0.1 reshape.86
  33.5 0.1 fusion.8
  33.6 0.1 fusion.9
  33.7 0.1 maximum_bitcast_fusion
  33.8 0.3 copy.6
  34.2 1.2 %reshape.87 = f32[2,16384]{1,0:T(2,128)} reshape(f32[2,1024,16]{2,1,0:T(8,128)S(1)} %copy.6) | data formatting | bytes 262144 | tf_op jit(solution)/shard_map/reshape | solution.py:271
  35.4 0.7 %fusion.2 = bf16[64,1024]{1,0:T(8,128)(2,1)} fusion(f32[32,1024]{1,0:T(8,128)S(1)} %get-tuple-element.29, f32[32,1024]{1,0:T(8,128)S(1)} %get-tuple-element.28, f32[1024]{0:T(1024)S(1)} %fusion.15, f32[1024]{0:T(1024)S(1)} %fusion.16), kind=kLoop, calls=%fused_computation.7 | loop fusion | flops 327680 | bytes 401408 | tf_op jit(solution)/shard_map/convert_element_type | solution.py:284
  (14 shorter events, 0.2 us)
Async XLA Ops:
  7.4 6.7 %collective-permute-start = (f32[256,128]{1,0:T(8,128)}, f32[256,128]{1,0:T(8,128)S(1)}, u32[]{:S(2)}, u32[]{:S(2)}) collective-permute-start(f32[256,128]{1,0:T(8,128)} %get-tuple-element.23), channel_id=1, source_target_pairs={{0,1},{1,0},{2,3},{3,2},{4,5},{5,4},{6,7},{7,6},{8,9},{9,8},{10,11... | collective-permute-start | bytes 393224 | tf_op jit(solution)/shard_map/ppermute | solution.py:174
  10.4 3.7 %copy-start = (f32[256,128]{1,0:T(8,128)S(1)}, f32[256,128]{1,0:T(8,128)}, u32[]{:S(2)}) copy-start(f32[256,128]{1,0:T(8,128)} %get-tuple-element.22) | copy-start | bytes 393220
  14.1 2.3 %copy-start.4 = (f32[16,128]{1,0:T(8,128)S(1)}, f32[16,128]{1,0:T(8,128)}, u32[]{:S(2)}) copy-start(f32[16,128]{1,0:T(8,128)} %get-tuple-element.25) | copy-start | bytes 24580
  14.1 4.0 %copy-start.3 = (bf16[32,1024]{1,0:T(8,128)(2,1)S(1)}, bf16[32,1024]{1,0:T(8,128)(2,1)}, u32[]{:S(2)}) copy-start(bf16[32,1024]{1,0:T(8,128)(2,1)} %get-tuple-element.27) | copy-start | bytes 196612
  14.2 5.9 %collective-permute-start.1 = (f32[64,128]{1,0:T(8,128)S(1)}, f32[64,128]{1,0:T(8,128)S(1)}, u32[]{:S(2)}, u32[]{:S(2)}) collective-permute-start(f32[64,128]{1,0:T(8,128)S(1)} %get-tuple-element.34), channel_id=1, source_target_pairs={{0,8},{8,0},{16,24},{24,16},{1,9},{9,1},{17,25},{25,17},{2,10},{10... | collective-permute-start | bytes 98312 | tf_op jit(solution)/shard_map/ppermute | solution.py:185
  14.3 5.8 %collective-permute-start.3 = (f32[64,128]{1,0:T(8,128)S(1)}, f32[64,128]{1,0:T(8,128)S(1)}, u32[]{:S(2)}, u32[]{:S(2)}) collective-permute-start(f32[64,128]{1,0:T(8,128)S(1)} %get-tuple-element.35), channel_id=1, source_target_pairs={{0,24},{8,16},{16,8},{24,0},{1,25},{9,17},{17,9},{25,1},{2,26},{10... | collective-permute-start | bytes 98312 | tf_op jit(solution)/shard_map/ppermute | solution.py:185
  16.1 4.0 %collective-permute-start.2 = (f32[64,128]{1,0:T(8,128)S(1)}, f32[64,128]{1,0:T(8,128)S(1)}, u32[]{:S(2)}, u32[]{:S(2)}) collective-permute-start(f32[64,128]{1,0:T(8,128)S(1)} %get-tuple-element.36), channel_id=1, source_target_pairs={{0,16},{8,24},{16,0},{24,8},{1,17},{9,25},{17,1},{25,9},{2,18},{10... | collective-permute-start | bytes 98312 | tf_op jit(solution)/shard_map/ppermute | solution.py:185
  16.4 3.7 %collective-permute-start.4 = (f32[16,128]{1,0:T(8,128)S(1)}, f32[16,128]{1,0:T(8,128)S(1)}, u32[]{:S(2)}, u32[]{:S(2)}) collective-permute-start(f32[16,128]{1,0:T(8,128)S(1)} %copy-done.4), channel_id=1, source_target_pairs={{0,1},{1,0},{2,3},{3,2},{4,5},{5,4},{6,7},{7,6},{8,9},{9,8},{10,11... | collective-permute-start | bytes 24584 | tf_op jit(solution)/shard_map/ppermute | solution.py:174
  18.1 6.4 %collective-permute-start.11 = (bf16[32,1024]{1,0:T(8,128)(2,1)S(1)}, bf16[32,1024]{1,0:T(8,128)(2,1)S(1)}, u32[]{:S(2)}, u32[]{:S(2)}) collective-permute-start(bf16[32,1024]{1,0:T(8,128)(2,1)S(1)} %copy-done.3), channel_id=1, source_target_pairs={{0,1},{1,0},{2,3},{3,2},{4,5},{5,4},{6,7},{7,6},{8,9},{9,8},{10,11... | collective-permute-start | bytes 196616 | tf_op jit(solution)/shard_map/ppermute | solution.py:174
  18.4 1.6 %copy-start.2 = (f32[16,128]{1,0:T(8,128)S(1)}, f32[16,128]{1,0:T(8,128)}, u32[]{:S(2)}) copy-start(f32[16,128]{1,0:T(8,128)} %get-tuple-element.24) | copy-start | bytes 24580
  20.1 5.1 %collective-permute-start.6 = (f32[80,128]{1,0:T(8,128)S(1)}, f32[80,128]{1,0:T(8,128)S(1)}, u32[]{:S(2)}, u32[]{:S(2)}) collective-permute-start(f32[80,128]{1,0:T(8,128)S(1)} %pad_maximum_fusion.2), channel_id=1, source_target_pairs={{0,4},{2,6},{4,0},{6,2},{1,5},{3,7},{5,1},{7,3},{8,12},{10,14},{12... | collective-permute-start | bytes 122888 | tf_op jit(solution)/shard_map/ppermute | solution.py:185
  23.0 5.8 %collective-permute-start.7 = (f32[80,128]{1,0:T(8,128)S(1)}, f32[80,128]{1,0:T(8,128)S(1)}, u32[]{:S(2)}, u32[]{:S(2)}) collective-permute-start(f32[80,128]{1,0:T(8,128)S(1)} %pad_maximum_fusion.2), channel_id=1, source_target_pairs={{0,6},{2,4},{4,2},{6,0},{1,7},{3,5},{5,3},{7,1},{8,14},{10,12},{12... | collective-permute-start | bytes 122888 | tf_op jit(solution)/shard_map/ppermute | solution.py:185
  24.3 4.5 %collective-permute-start.5 = (f32[80,128]{1,0:T(8,128)S(1)}, f32[80,128]{1,0:T(8,128)S(1)}, u32[]{:S(2)}, u32[]{:S(2)}) collective-permute-start(f32[80,128]{1,0:T(8,128)S(1)} %pad_maximum_fusion.2), channel_id=1, source_target_pairs={{0,2},{2,0},{4,6},{6,4},{1,3},{3,1},{5,7},{7,5},{8,10},{10,8},{12,... | collective-permute-start | bytes 122888 | tf_op jit(solution)/shard_map/ppermute | solution.py:185
  24.6 6.2 %copy-start.1 = (f32[32,1024]{1,0:T(8,128)S(1)}, f32[32,1024]{1,0:T(8,128)}, u32[]{:S(2)}) copy-start(f32[32,1024]{1,0:T(8,128)} %get-tuple-element.26) | copy-start | bytes 393220
  28.8 3.9 %collective-permute-start.10 = (f32[80,128]{1,0:T(8,128)S(1)}, f32[80,128]{1,0:T(8,128)S(1)}, u32[]{:S(2)}, u32[]{:S(2)}) collective-permute-start(f32[80,128]{1,0:T(8,128)S(1)} %add_add_fusion), channel_id=1, source_target_pairs={{0,24},{8,16},{16,8},{24,0},{1,25},{9,17},{17,9},{25,1},{2,26},{10... | collective-permute-start | bytes 122888 | tf_op jit(solution)/shard_map/ppermute | solution.py:185
  28.9 4.4 %collective-permute-start.9 = (f32[80,128]{1,0:T(8,128)S(1)}, f32[80,128]{1,0:T(8,128)S(1)}, u32[]{:S(2)}, u32[]{:S(2)}) collective-permute-start(f32[80,128]{1,0:T(8,128)S(1)} %add_add_fusion), channel_id=1, source_target_pairs={{0,16},{8,24},{16,0},{24,8},{1,17},{9,25},{17,1},{25,9},{2,18},{10... | collective-permute-start | bytes 122888 | tf_op jit(solution)/shard_map/ppermute | solution.py:185
  30.5 2.8 %collective-permute-start.8 = (f32[80,128]{1,0:T(8,128)S(1)}, f32[80,128]{1,0:T(8,128)S(1)}, u32[]{:S(2)}, u32[]{:S(2)}) collective-permute-start(f32[80,128]{1,0:T(8,128)S(1)} %add_add_fusion), channel_id=1, source_target_pairs={{0,8},{8,0},{16,24},{24,16},{1,9},{9,1},{17,25},{25,17},{2,10},{10... | collective-permute-start | bytes 122888 | tf_op jit(solution)/shard_map/ppermute | solution.py:185

commit v4 on v3

--- a/solution.py
+++ b/solution.py
@@ -83,11 +83,11 @@
         )
 
     def cells(step, carry):
-        for u in range(4):
-            one_cell(step * 4 + u)
+        for u in range(8):
+            one_cell(step * 8 + u)
         return carry
 
-    lax.fori_loop(0, rows // 4, cells, 0)
+    lax.fori_loop(0, rows // 8, cells, 0)
 
     own_high = HIGH // owners
     together = 4

time: 36.2 us -> 35.3 us (0.975)
  Pallas kernels: 10.2 us -> 9.3 us
    pallas_call x1, Pallas kernels: 6.77 us -> 5.85 us  [per_device(): pl.pallas_call(functools.partial(scatter_kernel, owners=owners), out_shap...]
where the time goes in v4:
time: 35.3 us; the launch traced here: 35.2 us
  starting transfers between devices  13.6 us (39%)
  Pallas kernels  9.3 us (26%)
  waiting for transfers between devices  8.55 us (24%)
  local copies, waits for them, and re-layouts  1.71 us (5%)
  other arithmetic  1.14 us (3%)
  between operations  0.83 us (2%)
    ppermute x9, starting transfers between devices, exchange(): return lax.ppermute(value, axis, [(s, s ^ d) for s in range(n)])  8.61 us
    ppermute x9, waiting for transfers between devices, exchange(): return lax.ppermute(value, axis, [(s, s ^ d) for s in range(n)])  6.69 us
    pallas_call x1, Pallas kernels, per_device(): pl.pallas_call(functools.partial(scatter_kernel, owners=owners), out_shap...  5.85 us
    ppermute x3, starting transfers between devices, shift(): return lax.ppermute(value, axis, [(s, (s + d) % n) for s in range(n)])  5.02 us
    pallas_call x1, Pallas kernels, per_device(): pl.pallas_call(functools.partial(select_kernel, owners=owners), out_shape...  3.45 us
    ppermute x3, waiting for transfers between devices, shift(): return lax.ppermute(value, axis, [(s, (s + d) % n) for s in range(n)])  1.86 us
    reshape x1, local copies, waits for them, and re-layouts, per_device(): gene_stats = jnp.stack([mean, variance]).transpose(0, 2, 1).reshape(2, -1)  1.23 us
  transfers between devices with their start and end apart: 12, of which 6 were waited for; matrix products, arithmetic and copies ran while one was open for 0% of the time, Pallas kernels for 10%

profile of v4, /device:TPU:0, one launch (start us, length us, event | category | flops | bytes accessed | tf_op | source)
XLA Modules:
  0.0 35.2 jit_solution(1948890119021045820)
XLA Ops:
  0.6 5.9 %scatter.1 = (f32[1024,128]{1,0:T(8,128)}, f32[32,128]{1,0:T(8,128)}, f32[256,128]{1,0:T(8,128)}, f32[256,128]{1,0:T(8,128)}) custom-call(s32[1]{0:T(128)} %bitcast.owner_ref, s32[32,2048]{1,0:T(8,128)} %columns_ref.1, s32[32,2048]{1,0:T(8,128)} %counts_ref.1, s32[1,32]{1,0:T(1,128)} %bitcast.62), custom_call_target="tpu_custom_call" | custom-call | tf_op jit(solution)/shard_map/scatter/pallas_call | solution.py:219
  6.5 3.0 %collective-permute-start = (f32[256,128]{1,0:T(8,128)}, f32[256,128]{1,0:T(8,128)S(1)}, u32[]{:S(2)}, u32[]{:S(2)}) collective-permute-start(f32[256,128]{1,0:T(8,128)} %get-tuple-element.23), channel_id=1, source_target_pairs={{0,1},{1,0},{2,3},{3,2},{4,5},{5,4},{6,7},{7,6},{8,9},{9,8},{10,11... | collective-permute-start | bytes 393224 | tf_op jit(solution)/shard_map/ppermute | solution.py:174
  9.5 0.0 copy-start
  9.5 3.5 %select.5 = (f32[32,1024]{1,0:T(8,128)}, bf16[32,1024]{1,0:T(8,128)(2,1)}, f32[16,128]{1,0:T(8,128)}, f32[16,128]{1,0:T(8,128)}) custom-call(s32[1]{0:T(128)} %bitcast.owner_ref, f32[1024,128]{1,0:T(8,128)} %get-tuple-element.16.compact_ref, f32[32,128]{1,0:T(8,128)} %get-tuple-element.17.scale_ref, s32[1,2048]{1,0:T(1,128)} %bitcast.61), custom_call_target="tpu_custom_call" | custom-call | tf_op jit(solution)/shard_map/select/pallas_call | solution.py:233
  12.9 0.2 collective-permute-done
  13.2 0.0 copy-done
  13.2 0.0 copy-start.4
  13.2 0.0 copy-start.3
  13.2 0.1 collective-permute-start.1
  13.3 1.8 %collective-permute-start.3 = (f32[64,128]{1,0:T(8,128)S(1)}, f32[64,128]{1,0:T(8,128)S(1)}, u32[]{:S(2)}, u32[]{:S(2)}) collective-permute-start(f32[64,128]{1,0:T(8,128)S(1)} %get-tuple-element.35), channel_id=1, source_target_pairs={{0,24},{8,16},{16,8},{24,0},{1,25},{9,17},{17,9},{25,1},{2,26},{10... | collective-permute-start | bytes 98312 | tf_op jit(solution)/shard_map/ppermute | solution.py:185
  15.1 0.3 collective-permute-start.2
  15.5 0.0 copy-done.4
  15.5 1.7 %collective-permute-start.4 = (f32[16,128]{1,0:T(8,128)S(1)}, f32[16,128]{1,0:T(8,128)S(1)}, u32[]{:S(2)}, u32[]{:S(2)}) collective-permute-start(f32[16,128]{1,0:T(8,128)S(1)} %copy-done.4), channel_id=1, source_target_pairs={{0,1},{1,0},{2,3},{3,2},{4,5},{5,4},{6,7},{7,6},{8,9},{9,8},{10,11... | collective-permute-start | bytes 24584 | tf_op jit(solution)/shard_map/ppermute | solution.py:174
  17.2 0.0 copy-done.3
  17.2 0.3 collective-permute-start.11
  17.5 0.0 copy-start.2
  17.5 1.6 %collective-permute-done.4 = f32[16,128]{1,0:T(8,128)S(1)} collective-permute-done((f32[16,128]{1,0:T(8,128)S(1)}, f32[16,128]{1,0:T(8,128)S(1)}, u32[]{:S(2)}, u32[]{:S(2)}) %collective-permute-start.4) | collective-permute-done | bytes 8224 | tf_op jit(solution)/shard_map/ppermute | solution.py:174
  19.1 0.0 copy-done.2
  19.1 0.0 collective-permute-done.1
  19.1 0.0 collective-permute-done.3
  19.1 0.0 collective-permute-done.2
  19.2 2.9 %collective-permute-start.6 = (f32[80,128]{1,0:T(8,128)S(1)}, f32[80,128]{1,0:T(8,128)S(1)}, u32[]{:S(2)}, u32[]{:S(2)}) collective-permute-start(f32[80,128]{1,0:T(8,128)S(1)} %pad_maximum_fusion.2), channel_id=1, source_target_pairs={{0,4},{2,6},{4,0},{6,2},{1,5},{3,7},{5,1},{7,3},{8,12},{10,14},{12... | collective-permute-start | bytes 122888 | tf_op jit(solution)/shard_map/ppermute | solution.py:185
  22.1 1.3 %collective-permute-start.7 = (f32[80,128]{1,0:T(8,128)S(1)}, f32[80,128]{1,0:T(8,128)S(1)}, u32[]{:S(2)}, u32[]{:S(2)}) collective-permute-start(f32[80,128]{1,0:T(8,128)S(1)} %pad_maximum_fusion.2), channel_id=1, source_target_pairs={{0,6},{2,4},{4,2},{6,0},{1,7},{3,5},{5,3},{7,1},{8,14},{10,12},{12... | collective-permute-start | bytes 122888 | tf_op jit(solution)/shard_map/ppermute | solution.py:185
  23.4 0.3 collective-permute-start.5
  23.7 0.0 collective-permute-done.11
  23.7 0.0 copy-start.1
  23.7 0.5 %collective-permute-done.6 = f32[80,128]{1,0:T(8,128)S(1)} collective-permute-done((f32[80,128]{1,0:T(8,128)S(1)}, f32[80,128]{1,0:T(8,128)S(1)}, u32[]{:S(2)}, u32[]{:S(2)}) %collective-permute-start.6) | collective-permute-done | bytes 40992 | tf_op jit(solution)/shard_map/ppermute | solution.py:185
  24.2 3.6 %collective-permute-done.7 = f32[80,128]{1,0:T(8,128)S(1)} collective-permute-done((f32[80,128]{1,0:T(8,128)S(1)}, f32[80,128]{1,0:T(8,128)S(1)}, u32[]{:S(2)}, u32[]{:S(2)}) %collective-permute-start.7) | collective-permute-done | bytes 40992 | tf_op jit(solution)/shard_map/ppermute | solution.py:185
  27.9 0.0 collective-permute-done.5
  27.9 0.1 collective-permute-start.10
  28.0 1.5 %collective-permute-start.9 = (f32[80,128]{1,0:T(8,128)S(1)}, f32[80,128]{1,0:T(8,128)S(1)}, u32[]{:S(2)}, u32[]{:S(2)}) collective-permute-start(f32[80,128]{1,0:T(8,128)S(1)} %add_add_fusion), channel_id=1, source_target_pairs={{0,16},{8,24},{16,0},{24,8},{1,17},{9,25},{17,1},{25,9},{2,18},{10... | collective-permute-start | bytes 122888 | tf_op jit(solution)/shard_map/ppermute | solution.py:185
  29.5 0.3 collective-permute-start.8
  29.8 0.0 copy-done.1
  29.8 0.1 fusion.6
  29.9 1.9 %collective-permute-done.10 = f32[80,128]{1,0:T(8,128)S(1)} collective-permute-done((f32[80,128]{1,0:T(8,128)S(1)}, f32[80,128]{1,0:T(8,128)S(1)}, u32[]{:S(2)}, u32[]{:S(2)}) %collective-permute-start.10) | collective-permute-done | bytes 40992 | tf_op jit(solution)/shard_map/ppermute | solution.py:185
  31.8 0.6 %collective-permute-done.9 = f32[80,128]{1,0:T(8,128)S(1)} collective-permute-done((f32[80,128]{1,0:T(8,128)S(1)}, f32[80,128]{1,0:T(8,128)S(1)}, u32[]{:S(2)}, u32[]{:S(2)}) %collective-permute-start.9) | collective-permute-done | bytes 40992 | tf_op jit(solution)/shard_map/ppermute | solution.py:185
  32.4 0.0 collective-permute-done.8
  32.5 0.1 reshape.86
  32.6 0.1 fusion.8
  32.7 0.1 fusion.9
  32.8 0.1 maximum_bitcast_fusion
  32.9 0.3 copy.6
  33.2 1.2 %reshape.87 = f32[2,16384]{1,0:T(2,128)} reshape(f32[2,1024,16]{2,1,0:T(8,128)S(1)} %copy.6) | data formatting | bytes 262144 | tf_op jit(solution)/shard_map/reshape | solution.py:271
  34.5 0.7 %fusion.2 = bf16[64,1024]{1,0:T(8,128)(2,1)} fusion(f32[32,1024]{1,0:T(8,128)S(1)} %get-tuple-element.29, f32[32,1024]{1,0:T(8,128)S(1)} %get-tuple-element.28, f32[1024]{0:T(1024)S(1)} %fusion.15, f32[1024]{0:T(1024)S(1)} %fusion.16), kind=kLoop, calls=%fused_computation.7 | loop fusion | flops 327680 | bytes 401408 | tf_op jit(solution)/shard_map/convert_element_type | solution.py:284
  (14 shorter events, 0.2 us)
Async XLA Ops:
  6.5 6.7 %collective-permute-start = (f32[256,128]{1,0:T(8,128)}, f32[256,128]{1,0:T(8,128)S(1)}, u32[]{:S(2)}, u32[]{:S(2)}) collective-permute-start(f32[256,128]{1,0:T(8,128)} %get-tuple-element.23), channel_id=1, source_target_pairs={{0,1},{1,0},{2,3},{3,2},{4,5},{5,4},{6,7},{7,6},{8,9},{9,8},{10,11... | collective-permute-start | bytes 393224 | tf_op jit(solution)/shard_map/ppermute | solution.py:174
  9.5 3.7 %copy-start = (f32[256,128]{1,0:T(8,128)S(1)}, f32[256,128]{1,0:T(8,128)}, u32[]{:S(2)}) copy-start(f32[256,128]{1,0:T(8,128)} %get-tuple-element.22) | copy-start | bytes 393220
  13.2 2.3 %copy-start.4 = (f32[16,128]{1,0:T(8,128)S(1)}, f32[16,128]{1,0:T(8,128)}, u32[]{:S(2)}) copy-start(f32[16,128]{1,0:T(8,128)} %get-tuple-element.25) | copy-start | bytes 24580
  13.2 4.0 %copy-start.3 = (bf16[32,1024]{1,0:T(8,128)(2,1)S(1)}, bf16[32,1024]{1,0:T(8,128)(2,1)}, u32[]{:S(2)}) copy-start(bf16[32,1024]{1,0:T(8,128)(2,1)} %get-tuple-element.27) | copy-start | bytes 196612
  13.2 5.9 %collective-permute-start.1 = (f32[64,128]{1,0:T(8,128)S(1)}, f32[64,128]{1,0:T(8,128)S(1)}, u32[]{:S(2)}, u32[]{:S(2)}) collective-permute-start(f32[64,128]{1,0:T(8,128)S(1)} %get-tuple-element.34), channel_id=1, source_target_pairs={{0,8},{8,0},{16,24},{24,16},{1,9},{9,1},{17,25},{25,17},{2,10},{10... | collective-permute-start | bytes 98312 | tf_op jit(solution)/shard_map/ppermute | solution.py:185
  13.3 5.8 %collective-permute-start.3 = (f32[64,128]{1,0:T(8,128)S(1)}, f32[64,128]{1,0:T(8,128)S(1)}, u32[]{:S(2)}, u32[]{:S(2)}) collective-permute-start(f32[64,128]{1,0:T(8,128)S(1)} %get-tuple-element.35), channel_id=1, source_target_pairs={{0,24},{8,16},{16,8},{24,0},{1,25},{9,17},{17,9},{25,1},{2,26},{10... | collective-permute-start | bytes 98312 | tf_op jit(solution)/shard_map/ppermute | solution.py:185
  15.1 4.0 %collective-permute-start.2 = (f32[64,128]{1,0:T(8,128)S(1)}, f32[64,128]{1,0:T(8,128)S(1)}, u32[]{:S(2)}, u32[]{:S(2)}) collective-permute-start(f32[64,128]{1,0:T(8,128)S(1)} %get-tuple-element.36), channel_id=1, source_target_pairs={{0,16},{8,24},{16,0},{24,8},{1,17},{9,25},{17,1},{25,9},{2,18},{10... | collective-permute-start | bytes 98312 | tf_op jit(solution)/shard_map/ppermute | solution.py:185
  15.5 3.7 %collective-permute-start.4 = (f32[16,128]{1,0:T(8,128)S(1)}, f32[16,128]{1,0:T(8,128)S(1)}, u32[]{:S(2)}, u32[]{:S(2)}) collective-permute-start(f32[16,128]{1,0:T(8,128)S(1)} %copy-done.4), channel_id=1, source_target_pairs={{0,1},{1,0},{2,3},{3,2},{4,5},{5,4},{6,7},{7,6},{8,9},{9,8},{10,11... | collective-permute-start | bytes 24584 | tf_op jit(solution)/shard_map/ppermute | solution.py:174
  17.2 6.5 %collective-permute-start.11 = (bf16[32,1024]{1,0:T(8,128)(2,1)S(1)}, bf16[32,1024]{1,0:T(8,128)(2,1)S(1)}, u32[]{:S(2)}, u32[]{:S(2)}) collective-permute-start(bf16[32,1024]{1,0:T(8,128)(2,1)S(1)} %copy-done.3), channel_id=1, source_target_pairs={{0,1},{1,0},{2,3},{3,2},{4,5},{5,4},{6,7},{7,6},{8,9},{9,8},{10,11... | collective-permute-start | bytes 196616 | tf_op jit(solution)/shard_map/ppermute | solution.py:174
  17.5 1.6 %copy-start.2 = (f32[16,128]{1,0:T(8,128)S(1)}, f32[16,128]{1,0:T(8,128)}, u32[]{:S(2)}) copy-start(f32[16,128]{1,0:T(8,128)} %get-tuple-element.24) | copy-start | bytes 24580
  19.2 5.1 %collective-permute-start.6 = (f32[80,128]{1,0:T(8,128)S(1)}, f32[80,128]{1,0:T(8,128)S(1)}, u32[]{:S(2)}, u32[]{:S(2)}) collective-permute-start(f32[80,128]{1,0:T(8,128)S(1)} %pad_maximum_fusion.2), channel_id=1, source_target_pairs={{0,4},{2,6},{4,0},{6,2},{1,5},{3,7},{5,1},{7,3},{8,12},{10,14},{12... | collective-permute-start | bytes 122888 | tf_op jit(solution)/shard_map/ppermute | solution.py:185
  22.1 5.8 %collective-permute-start.7 = (f32[80,128]{1,0:T(8,128)S(1)}, f32[80,128]{1,0:T(8,128)S(1)}, u32[]{:S(2)}, u32[]{:S(2)}) collective-permute-start(f32[80,128]{1,0:T(8,128)S(1)} %pad_maximum_fusion.2), channel_id=1, source_target_pairs={{0,6},{2,4},{4,2},{6,0},{1,7},{3,5},{5,3},{7,1},{8,14},{10,12},{12... | collective-permute-start | bytes 122888 | tf_op jit(solution)/shard_map/ppermute | solution.py:185
  23.4 4.5 %collective-permute-start.5 = (f32[80,128]{1,0:T(8,128)S(1)}, f32[80,128]{1,0:T(8,128)S(1)}, u32[]{:S(2)}, u32[]{:S(2)}) collective-permute-start(f32[80,128]{1,0:T(8,128)S(1)} %pad_maximum_fusion.2), channel_id=1, source_target_pairs={{0,2},{2,0},{4,6},{6,4},{1,3},{3,1},{5,7},{7,5},{8,10},{10,8},{12,... | collective-permute-start | bytes 122888 | tf_op jit(solution)/shard_map/ppermute | solution.py:185
  23.7 6.1 %copy-start.1 = (f32[32,1024]{1,0:T(8,128)S(1)}, f32[32,1024]{1,0:T(8,128)}, u32[]{:S(2)}) copy-start(f32[32,1024]{1,0:T(8,128)} %get-tuple-element.26) | copy-start | bytes 393220
  27.9 3.9 %collective-permute-start.10 = (f32[80,128]{1,0:T(8,128)S(1)}, f32[80,128]{1,0:T(8,128)S(1)}, u32[]{:S(2)}, u32[]{:S(2)}) collective-permute-start(f32[80,128]{1,0:T(8,128)S(1)} %add_add_fusion), channel_id=1, source_target_pairs={{0,24},{8,16},{16,8},{24,0},{1,25},{9,17},{17,9},{25,1},{2,26},{10... | collective-permute-start | bytes 122888 | tf_op jit(solution)/shard_map/ppermute | solution.py:185
  28.0 4.4 %collective-permute-start.9 = (f32[80,128]{1,0:T(8,128)S(1)}, f32[80,128]{1,0:T(8,128)S(1)}, u32[]{:S(2)}, u32[]{:S(2)}) collective-permute-start(f32[80,128]{1,0:T(8,128)S(1)} %add_add_fusion), channel_id=1, source_target_pairs={{0,16},{8,24},{16,0},{24,8},{1,17},{9,25},{17,1},{25,9},{2,18},{10... | collective-permute-start | bytes 122888 | tf_op jit(solution)/shard_map/ppermute | solution.py:185
  29.5 2.9 %collective-permute-start.8 = (f32[80,128]{1,0:T(8,128)S(1)}, f32[80,128]{1,0:T(8,128)S(1)}, u32[]{:S(2)}, u32[]{:S(2)}) collective-permute-start(f32[80,128]{1,0:T(8,128)S(1)} %add_add_fusion), channel_id=1, source_target_pairs={{0,8},{8,0},{16,24},{24,16},{1,9},{9,1},{17,25},{25,17},{2,10},{10... | collective-permute-start | bytes 122888 | tf_op jit(solution)/shard_map/ppermute | solution.py:185
